TPU v7x, 256 devices: a whole 4x4x8 slice. The times are simulated.
256 devices in a mesh: gx: 8 (over y, core), gy: 32 (over z, x).
Axes of the slice: x: 4, y: 4, z: 8, core: 2. Of those that a mesh axis runs over, the one named last changes fastest.
Arguments:
- tokens: bfloat16 [1024, 4096], P('gy', 'gx'), may hold values from -140 to 140
- cotangent: bfloat16 [1024, 4096], P('gy', 'gx'), may hold values from -6 to 6
- gate_weight: bfloat16 [4096, 14336], P('gx', 'gy'), may hold values from -5 to 5
- up_weight: bfloat16 [4096, 14336], P('gx', 'gy'), may hold values from -5 to 5
- down_weight: bfloat16 [14336, 4096], P('gy', 'gx'), may hold values from -5 to 5
Outputs:
- output: bfloat16 [1024, 4096], P('gy', 'gx')
- input_grad: bfloat16 [1024, 4096], P('gy', 'gx')
- gate_grad: bfloat16 [4096, 14336], P('gx', 'gy')
- up_grad: bfloat16 [4096, 14336], P('gx', 'gy')
- down_grad: bfloat16 [14336, 4096], P('gy', 'gx')
All inputs are finite; a program needn't handle non-finite values.
Results may differ from a plain program's by a relative error of at most 0.005.
The roundings to bfloat16 on the way count: a program that leaves them out, or rounds other values in their place, can miss the bound.
Values may be sent and summed in bfloat16 or wider, within the bound.
A program may use at most 64 MiB of HBM per device.

v0:
```python
import jax
import jax.numpy as jnp
from jax import lax
from jax.sharding import Mesh
from jax.sharding import PartitionSpec as P

ROT_BLOCK = 128
HID_BLOCK = 64
GX_GY = ("gx_0", "gx_1", "gy_0", "gy_1")
GY = ("gy_0", "gy_1")
GX = ("gx_0", "gx_1")


fp_top = 448.0
tiny = 1e-06


def by_axis(shard, axes):
    for axis in axes:
        shard = lax.pmax(shard, axis)
    return shard


def gathered_by_axis(shard, axes, dim):
    if not axes:
        return shard
    nearer = lax.all_gather(shard, axes[-1], axis=dim, tiled=True)
    return gathered_by_axis(nearer, axes[:-1], dim)


def copy_for_each(shard, axis):
    copies = jnp.broadcast_to(shard, (lax.axis_size(axis), *shard.shape))
    return lax.all_to_all(copies, axis, split_axis=0, concat_axis=0, tiled=True)


def over_copies(shard, axis):
    return copy_for_each(shard, axis).max(axis=0)


def cut_along(shard, dim, length):
    lengths = shard.shape
    parts = shard.reshape(*lengths[:dim], length, lengths[dim] // length, *lengths[dim + 1 :])
    return jnp.moveaxis(parts, dim, 0)


def sum_at_owner(shard, axis, dim):
    parts = cut_along(shard, dim, lax.axis_size(axis))
    arrived = lax.all_to_all(parts, axis, split_axis=0, concat_axis=0, tiled=True)
    return arrived.sum(axis=0)


def joined_along(parts, dim):
    parts = jnp.moveaxis(parts, 0, dim)
    lengths = parts.shape
    return parts.reshape(*lengths[:dim], lengths[dim] * lengths[dim + 1], *lengths[dim + 2 :])


def gather_directly(shard, axis, dim):
    parts = copy_for_each(shard, axis)
    return joined_along(parts, dim)


def own_rows(running, axes):
    for axis in axes:
        running = lax.psum_scatter(running, axis, scatter_dimension=0, tiled=True)
    return running


def sent_together(arrays, axis, dim, along):
    both = jnp.concatenate(arrays, axis=along)
    out, at, outs = (lax.all_gather(both, axis, axis=dim, tiled=True), 0, [])
    for a in arrays:
        outs.append(lax.slice_in_dim(out, at, at + a.shape[along], axis=along))
        at += a.shape[along]
    return tuple(outs)


def hadamard_table(block_size):
    row_ids = jnp.arange(block_size, dtype=jnp.int32)[:, None]
    col_ids = jnp.arange(block_size, dtype=jnp.int32)[None, :]
    shared = row_ids & col_ids
    parity = jnp.zeros((block_size, block_size), jnp.int32)
    for bit_pos in range(max(block_size.bit_length() - 1, 1)):
        parity = parity + (shared >> bit_pos & 1)
    return (1 - 2 * (parity % 2)).astype(jnp.float32)


def rotate_cols(matrix, block_size):
    row_total, col_total = matrix.shape
    table = hadamard_table(block_size)
    blocks = matrix.reshape(row_total, col_total // block_size, block_size)
    if matrix.dtype == jnp.bfloat16:
        turned = jnp.einsum(
            "rbk,kl->rbl", blocks, table.astype(jnp.bfloat16), preferred_element_type=jnp.float32
        )
    else:
        turned = jnp.einsum("rbk,kl->rbl", blocks, table, precision=lax.Precision.HIGHEST)
    return turned.reshape(row_total, col_total) * block_size ** (-0.5)


def rotate_rows(matrix, block_size):
    row_total, col_total = matrix.shape
    table = hadamard_table(block_size)
    blocks = matrix.reshape(row_total // block_size, block_size, col_total)
    if matrix.dtype == jnp.bfloat16:
        turned = jnp.einsum(
            "kl,bkc->blc", table.astype(jnp.bfloat16), blocks, preferred_element_type=jnp.float32
        )
    else:
        turned = jnp.einsum("kl,bkc->blc", table, blocks, precision=lax.Precision.HIGHEST)
    return turned.reshape(row_total, col_total) * block_size ** (-0.5)


def soft_cast(values, top):
    return (fp_top * jnp.tanh(values / (top + tiny))).astype(jnp.bfloat16)


def peak(values):
    return jnp.max(jnp.abs(values))


def contract_rows(left_mat, right_mat):
    return lax.dot_general(
        left_mat, right_mat, (((0,), (0,)), ((), ())), preferred_element_type=jnp.float32
    )


def contract_cols(left_mat, right_mat):
    return lax.dot_general(
        left_mat, right_mat, (((1,), (1,)), ((), ())), preferred_element_type=jnp.float32
    )


def shards(tokens, cotangent, gate_weight, up_weight, down_weight):
    gate_rot = rotate_rows(gate_weight, ROT_BLOCK)
    up_rot = rotate_rows(up_weight, ROT_BLOCK)
    down_rot = rotate_rows(down_weight, HID_BLOCK)
    gate_peak, up_peak, down_peak = (
        by_axis(peak(gate_rot), GX_GY),
        by_axis(peak(up_rot), GX_GY),
        by_axis(peak(down_rot), GX_GY),
    )
    gate_cast = soft_cast(gate_rot, gate_peak)
    up_cast = soft_cast(up_rot, up_peak)
    down_cast = soft_cast(down_rot, down_peak)
    hid_width = gate_weight.shape[1]
    all_tokens = gathered_by_axis(tokens, GY, 0)
    token_rot = rotate_cols(all_tokens, ROT_BLOCK)
    token_peak = over_copies(peak(token_rot), GX)
    token_cast = soft_cast(token_rot, token_peak)
    weight_pair = jnp.concatenate([gate_cast, up_cast], axis=1)
    picked = token_cast
    paired = sum_at_owner(jnp.dot(picked, weight_pair, preferred_element_type=jnp.float32), GX, 0)
    gate_pre = paired[:, :hid_width] * (token_peak * gate_peak / (fp_top * fp_top))
    up_pre = paired[:, hid_width:] * (token_peak * up_peak / (fp_top * fp_top))
    hidden = (jax.nn.silu(gate_pre) * up_pre).astype(jnp.bfloat16)
    all_hidden = gather_directly(hidden, GX, 0)
    hidden_rot = rotate_cols(all_hidden, HID_BLOCK)
    hidden_peak = over_copies(peak(hidden_rot), GY)
    hidden_cast = soft_cast(hidden_rot, hidden_peak)
    picked = hidden_cast
    out_sum = own_rows(jnp.dot(picked, down_cast, preferred_element_type=jnp.float32), GY)
    output = (out_sum * (hidden_peak * down_peak / (fp_top * fp_top))).astype(jnp.bfloat16)
    all_cot = gathered_by_axis(cotangent, GY, 0)
    down_grad = rotate_rows(
        contract_rows(hidden_cast, all_cot) * (hidden_peak / fp_top), HID_BLOCK
    ).astype(jnp.bfloat16)
    picked = all_cot
    back_sum = sum_at_owner(contract_cols(picked, down_cast), GX, 0)
    hidden_grad = rotate_cols(back_sum * (down_peak / fp_top), HID_BLOCK)
    sigmoid_gate = jax.nn.sigmoid(gate_pre)
    gate_act = (
        hidden_grad * up_pre * sigmoid_gate * (1.0 + gate_pre * (1.0 - sigmoid_gate))
    ).astype(jnp.bfloat16)
    up_act = (hidden_grad * gate_pre * sigmoid_gate).astype(jnp.bfloat16)
    all_gate_act, all_up_act = sent_together((gate_act, up_act), GX, 0, 1)
    gate_grad = rotate_rows(
        contract_rows(token_cast, all_gate_act) * (token_peak / fp_top), ROT_BLOCK
    ).astype(jnp.bfloat16)
    up_grad = rotate_rows(
        contract_rows(token_cast, all_up_act) * (token_peak / fp_top), ROT_BLOCK
    ).astype(jnp.bfloat16)
    input_sum = sum_at_owner(
        contract_cols(all_gate_act, gate_cast) * (gate_peak / fp_top)
        + contract_cols(all_up_act, up_cast) * (up_peak / fp_top),
        GY,
        0,
    )
    input_grad = rotate_cols(input_sum, ROT_BLOCK).astype(jnp.bfloat16)
    return (output, input_grad, gate_grad, up_grad, down_grad)


def solution(mesh):
    split = Mesh(mesh.devices.reshape(4, 2, 8, 4), ("gx_0", "gx_1", "gy_0", "gy_1"))
    placed = (P(GY, GX), P(GY, GX), P(GX, GY), P(GX, GY), P(GY, GX))
    return jax.shard_map(
        shards,
        mesh=split,
        in_specs=placed,
        out_specs=(P(GY, GX), P(GY, GX), P(GX, GY), P(GX, GY), P(GY, GX)),
        check_vma=False,
    )
```

profile of v0, /device:TPU:16, one launch (start us, length us, event | category | flops | bytes accessed | tf_op | source)
XLA Modules:
  0.0 335.8 jit_solution(2199470831104127422)
XLA Ops:
  7.2 12.7 %all_gather.15 = bf16[128,512]{1,0:T(8,128)(2,1)S(1)} all-gather(bf16[32,512]{1,0:T(8,128)(2,1)} %param.5), channel_id=1, replica_groups=mesh['gx_0'=4,'gx_1'=2,'gy_0'=8,'gy_1'=4] {'gy_1'}, dimensions={0}, use_global_device_ids=true | all-gather | bytes 163840 | tf_op jit(solution)/shard_map/all_gather | solution.py:27
  20.8 13.5 %all_gather.17 = bf16[128,512]{1,0:T(8,128)(2,1)} all-gather(bf16[32,512]{1,0:T(8,128)(2,1)} %param.6), channel_id=1, replica_groups=mesh['gx_0'=4,'gx_1'=2,'gy_0'=8,'gy_1'=4] {'gy_1'}, dimensions={0}, use_global_device_ids=true | all-gather | bytes 163840 | tf_op jit(solution)/shard_map/all_gather | solution.py:27
  34.3 2.9 abs_reduce_fusion.3
  37.2 1.9 abs_reduce_fusion.4
  40.0 9.0 %all-reduce.2 = (f32[]{:T(128)}, f32[]{:T(128)}, f32[]{:T(128)}) all-reduce(f32[]{:T(128)} %get-tuple-element.22, f32[]{:T(128)} %get-tuple-element.24, f32[]{:T(128)} %get-tuple-element.26), channel_id=1, replica_groups=mesh['gx_0'=4,'gx_1'=2,'gy_0'=8,'gy_1'=4] {'gx_0'}, use_global_device_ids=true, to_apply=%region_8.9 | all-reduce | flops 3 | bytes 24 | tf_op jit(solution)/shard_map/pmax | solution.py:20
  49.0 3.1 all-reduce.3
  52.1 20.6 %all-reduce = (f32[]{:T(128)}, f32[]{:T(128)}, f32[]{:T(128)}) all-reduce(f32[]{:T(128)} %get-tuple-element.14, f32[]{:T(128)} %get-tuple-element.15, f32[]{:T(128)} %get-tuple-element.16), channel_id=1, replica_groups=mesh['gx_0'=4,'gx_1'=2,'gy_0'=8,'gy_1'=4] {'gy_0'}, use_global_device_ids=true, to_apply=%region_10.11 | all-reduce | flops 3 | bytes 24 | tf_op jit(solution)/shard_map/pmax | solution.py:20
  72.7 10.2 %all-reduce.1 = (f32[]{:T(128)}, f32[]{:T(128)}, f32[]{:T(128)}) all-reduce(f32[]{:T(128)} %get-tuple-element.5, f32[]{:T(128)} %get-tuple-element.6, f32[]{:T(128)} %get-tuple-element.7), channel_id=1, replica_groups=mesh['gx_0'=4,'gx_1'=2,'gy_0'=8,'gy_1'=4] {'gy_1'}, use_global_device_ids=true, to_apply=%region_11.12 | all-reduce | flops 3 | bytes 24 | tf_op jit(solution)/shard_map/pmax | solution.py:20
  83.7 2.5 abs_reduce_fusion
  87.4 5.9 %all-to-all-start = ((f32[8,1,1]{2,1,0:T(1,128)}), f32[8,1,1]{2,1,0:T(1,128)S(1)}, u32[]{:S(2)}, u32[]{:S(2)}) async-start(f32[8,1,1]{2,1,0:T(1,128)} %broadcast_in_dim.6), calls=%async_computation | async-start | bytes 8192 | tf_op jit(solution)/shard_map/all_to_all | solution.py:33
  93.3 8.4 %all-gather.6.cloned.1.call-done = bf16[1024,512]{1,0:T(8,128)(2,1)} async-done(((bf16[128,512]{1,0:T(8,128)(2,1)}), bf16[1024,512]{1,0:T(8,128)(2,1)}) %all-gather.6.cloned.1.call-update) | async-done | bytes 1048592 | tf_op jit(solution)/shard_map/all_gather | solution.py:27
  101.7 1.9 convolution_bitcast_fusion.1
  105.0 4.8 %all-to-all-start.4 = ((f32[8,128,448]{1,2,0:T(8,128)}), f32[8,128,448]{1,2,0:T(8,128)}, u32[]{:S(2)}, u32[]{:S(2)}) async-start(f32[8,128,448]{1,2,0:T(8,128)} %bitcast.164), calls=%async_computation.6 | async-start | bytes 3670016 | tf_op jit(solution)/shard_map/all_to_all | solution.py:48
  117.9 3.1 fusion.9
  121.0 10.2 %all-to-all-done.4 = f32[8,128,448]{1,2,0:T(8,128)} async-done(((f32[8,128,448]{1,2,0:T(8,128)}), f32[8,128,448]{1,2,0:T(8,128)}, u32[]{:S(2)}, u32[]{:S(2)}) %all-to-all-start.4) | async-done | bytes 1835040 | tf_op jit(solution)/shard_map/all_to_all | solution.py:48
  131.1 7.6 %all-to-all-start.1 = ((f32[8,128,896]{2,1,0:T(8,128)}), f32[8,128,896]{2,1,0:T(8,128)}, u32[]{:S(2)}, u32[]{:S(2)}) async-start(f32[8,128,896]{2,1,0:T(8,128)} %fusion.9), calls=%async_computation.1 | async-start | bytes 7340032 | tf_op jit(solution)/shard_map/all_to_all | solution.py:48
  141.8 1.6 reduce_sum.28
  143.9 35.8 %all-to-all-done.1 = f32[8,128,896]{2,1,0:T(8,128)} async-done(((f32[8,128,896]{2,1,0:T(8,128)}), f32[8,128,896]{2,1,0:T(8,128)}, u32[]{:S(2)}, u32[]{:S(2)}) %all-to-all-start.1) | async-done | bytes 3670048 | tf_op jit(solution)/shard_map/all_to_all | solution.py:48
  179.7 2.3 reduce_sum.27
  183.4 19.9 %all_to_all.32 = bf16[8,128,448]{1,2,0:T(8,128)(2,1)S(1)} all-to-all(bf16[8,128,448]{1,2,0:T(8,128)(2,1)S(1)} %broadcast_in_dim.7), channel_id=1, replica_groups=mesh['gx_0'=4,'gx_1'=2,'gy_0'=8,'gy_1'=4] {'gx_0','gx_1'}, dimensions={0} | all-to-all | bytes 1835008 | tf_op jit(solution)/shard_map/all_to_all | solution.py:33
  206.0 16.5 %all_to_all.33 = f32[32,1,1]{2,1,0:T(1,128)S(1)} all-to-all(f32[32,1,1]{2,1,0:T(1,128)S(1)} %broadcast_in_dim.8), channel_id=1, replica_groups=mesh['gx_0'=4,'gx_1'=2,'gy_0'=8,'gy_1'=4] {'gy_0','gy_1'}, dimensions={0} | all-to-all | bytes 256 | tf_op jit(solution)/shard_map/all_to_all | solution.py:33
  225.2 2.1 convolution_bitcast_fusion
  228.7 2.1 fusion.20
  230.8 2.1 multiply_add_fusion
  233.0 4.1 %all-to-all-start.5 = ((f32[32,32,512]{2,1,0:T(8,128)}), f32[32,32,512]{2,1,0:T(8,128)S(1)}, u32[]{:S(2)}, u32[]{:S(2)}) async-start(f32[32,32,512]{2,1,0:T(8,128)} %bitcast.169), calls=%async_computation.7 | async-start | bytes 4194304 | tf_op jit(solution)/shard_map/all_to_all | solution.py:48
  239.8 2.0 convolution_multiply_fusion.1
  241.8 1.8 fusion.4
  243.6 1.6 fusion.1
  245.9 53.2 %reduce-scatter.3.cloned.1.call-done = f32[128,512]{1,0:T(8,128)} async-done(((f32[1024,512]{1,0:T(8,128)}), f32[128,512]{1,0:T(8,128)}) %reduce-scatter.3.cloned.1.call-update) | async-done | bytes 262160 | tf_op jit(solution)/shard_map/reduce_scatter | solution.py:65
  299.1 2.1 fusion.6
  303.2 23.6 %reduce-scatter.5.cloned.1.call-done = f32[32,512]{1,0:T(8,128)} async-done(((f32[128,512]{1,0:T(8,128)}), f32[32,512]{1,0:T(8,128)}) %reduce-scatter.5.cloned.1.call-update) | async-done | bytes 65552 | tf_op jit(solution)/shard_map/reduce_scatter | solution.py:65
  326.8 1.5 multiply_convert_fusion.6
  (72 shorter events, 20.9 us)
Async XLA Ops:
  7.2 31.9 %copy-start = (bf16[448,512]{1,0:T(8,128)(2,1)S(1)}, bf16[448,512]{1,0:T(8,128)(2,1)}, u32[]{:S(2)}) copy-start(bf16[448,512]{1,0:T(8,128)(2,1)} %param.9) | copy-start | bytes 1376260
  7.2 30.0 %copy-start.12 = (bf16[512,448]{0,1:T(8,128)(2,1)S(1)}, bf16[512,448]{0,1:T(8,128)(2,1)}, u32[]{:S(2)}) copy-start(bf16[512,448]{0,1:T(8,128)(2,1)} %param.7) | copy-start | bytes 1376260
  7.2 76.5 %all-gather.4.cloned.1.call-start = ((), (), s32[]{:S(2)}) async-start(), calls=%async_computation.8 | async-start | bytes 1179648 | tf_op jit(solution)/shard_map/all_gather | solution.py:27
  20.7 81.0 %all-gather.6.cloned.1.call-start = ((), (), s32[]{:S(2)}) async-start(), calls=%async_computation.11 | async-start | bytes 1179648 | tf_op jit(solution)/shard_map/all_gather | solution.py:27
  83.6 20.0 %copy-start.4 = (bf16[64,7,512]{2,0,1:T(8,128)(2,1)}, bf16[64,7,512]{2,0,1:T(8,128)(2,1)S(1)}, u32[]{:S(2)}) copy-start(bf16[64,7,512]{2,0,1:T(8,128)(2,1)S(1)} %multiply_convert_fusion.2) | copy-start | bytes 1376260
  87.4 17.6 %all-to-all-start = ((f32[8,1,1]{2,1,0:T(1,128)}), f32[8,1,1]{2,1,0:T(1,128)S(1)}, u32[]{:S(2)}, u32[]{:S(2)}) async-start(f32[8,1,1]{2,1,0:T(1,128)} %broadcast_in_dim.6), calls=%async_computation | async-start | bytes 8192 | tf_op jit(solution)/shard_map/all_to_all | solution.py:33
  105.0 26.1 %all-to-all-start.4 = ((f32[8,128,448]{1,2,0:T(8,128)}), f32[8,128,448]{1,2,0:T(8,128)}, u32[]{:S(2)}, u32[]{:S(2)}) async-start(f32[8,128,448]{1,2,0:T(8,128)} %bitcast.164), calls=%async_computation.6 | async-start | bytes 3670016 | tf_op jit(solution)/shard_map/all_to_all | solution.py:48
  116.2 1.6 copy-start.3
  116.6 1.0 copy-start.1
  131.1 48.5 %all-to-all-start.1 = ((f32[8,128,896]{2,1,0:T(8,128)}), f32[8,128,896]{2,1,0:T(8,128)}, u32[]{:S(2)}, u32[]{:S(2)}) async-start(f32[8,128,896]{2,1,0:T(8,128)} %fusion.9), calls=%async_computation.1 | async-start | bytes 7340032 | tf_op jit(solution)/shard_map/all_to_all | solution.py:48
  138.7 90.0 %all-gather.8.cloned.1.call-start = ((), (), s32[]{:S(2)}) async-start(), calls=%async_computation.12 | async-start | bytes 2064384 | tf_op jit(solution)/shard_map/all_gather | solution.py:71
  183.2 115.8 %reduce-scatter.3.cloned.1.call-start = ((), (), s32[]{:S(2)}) async-start(), calls=%async_computation.9 | async-start | bytes 2359296 | tf_op jit(solution)/shard_map/reduce_scatter | solution.py:65
  205.3 19.8 %copy-start.5 = (bf16[64,7,512]{2,0,1:T(8,128)(2,1)S(1)}, bf16[64,7,512]{2,0,1:T(8,128)(2,1)}, u32[]{:S(2)}) copy-start(bf16[64,7,512]{2,0,1:T(8,128)(2,1)} %copy-done.4) | copy-start | bytes 1376260
  224.2 0.9 copy-start.8
  227.2 1.4 copy-start.7
  228.6 2.2 copy-start.6
  228.7 2.1 copy-start.10
  233.0 6.8 %copy-start.9 = (bf16[1024,7,64]{0,2,1:T(8,128)(2,1)S(1)}, bf16[1024,7,64]{0,2,1:T(8,128)(2,1)}, u32[]{:S(2)}) copy-start(bf16[1024,7,64]{0,2,1:T(8,128)(2,1)} %copy-done.8) | copy-start | bytes 2752516
  233.0 95.3 %all-to-all-start.5 = ((f32[32,32,512]{2,1,0:T(8,128)}), f32[32,32,512]{2,1,0:T(8,128)S(1)}, u32[]{:S(2)}, u32[]{:S(2)}) async-start(f32[32,32,512]{2,1,0:T(8,128)} %bitcast.169), calls=%async_computation.7 | async-start | bytes 4194304 | tf_op jit(solution)/shard_map/all_to_all | solution.py:48
  237.1 89.7 %reduce-scatter.5.cloned.1.call-start = ((), (), s32[]{:S(2)}) async-start(), calls=%async_computation.10 | async-start | bytes 327680 | tf_op jit(solution)/shard_map/reduce_scatter | solution.py:65
  239.7 3.8 %copy-start.2 = (bf16[128,1024,4]{1,0,2:T(8,128)(2,1)S(1)}, bf16[128,1024,4]{1,0,2:T(8,128)(2,1)}, u32[]{:S(2)}) copy-start(bf16[128,1024,4]{1,0,2:T(8,128)(2,1)} %copy-done.1) | copy-start | bytes 3145732
  239.8 3.8 %copy-start.11 = (bf16[1024,896]{0,1:T(8,128)(2,1)S(1)}, bf16[1024,896]{0,1:T(8,128)(2,1)}, u32[]{:S(2)}) copy-start(bf16[1024,896]{0,1:T(8,128)(2,1)} %all-gather.8.cloned.1.call-done) | copy-start | bytes 5505028
Sparse Core Ops, SparseCore 0:
  20.8 41.4 all-gather.3
  64.1 37.5 all-gather.5
  183.3 31.4 all-gather.7
  227.4 71.6 reduce-scatter.2
  301.4 25.3 reduce-scatter.4
where the time goes:
time: 337 us; the launch traced here: 336 us
  waiting for transfers between devices  131 us (39%)
  blocking collectives  105 us (31%)
  matrix products  30.4 us (9%)
  between operations  24.4 us (7%)
  starting transfers between devices  22.6 us (7%)
  other arithmetic  11.1 us (3%)
  local copies, waits for them, and re-layouts  10.6 us (3%)
    reduce_scatter x2, waiting for transfers between devices, own_rows(): running = lax.psum_scatter(running, axis, scatter_dimension=0, tiled=True)  76.8 us
    all_to_all x3, waiting for transfers between devices, sum_at_owner(): lax.all_to_all(parts, axis, split_axis=0, concat_axis=0, tiled=True)  45.9 us
    pmax x4, blocking collectives, by_axis(): shard = lax.pmax(shard, axis)  42.9 us
    all_to_all x2, blocking collectives, copy_for_each(): return lax.all_to_all(copies, axis, split_axis=0, concat_axis=0, tiled=True)  36.4 us
    all_gather x2, blocking collectives, gathered_by_axis(): nearer = lax.all_gather(shard, axes[-1], axis=dim, tiled=True)  26.2 us
    all_to_all x3, starting transfers between devices, sum_at_owner(): lax.all_to_all(parts, axis, split_axis=0, concat_axis=0, tiled=True)  16.5 us
    all_gather x2, waiting for transfers between devices, gathered_by_axis(): nearer = lax.all_gather(shard, axes[-1], axis=dim, tiled=True)  8.41 us
  transfers between devices with their start and end apart: 9, of which 5 were waited for; matrix products, arithmetic and copies ran while one was open for 13% of the time, Pallas kernels for 0%

commit v1 on v0

v1 whole, which is shorter than its diff:
```python
import functools

import jax
import jax.numpy as jnp
from jax import lax
from jax.experimental import pallas as pl
from jax.experimental.pallas import tpu as pltpu
from jax.sharding import Mesh
from jax.sharding import PartitionSpec as P

GY = ("gy_0", "gy_1")
GX = ("gx_0", "gx_1")
NY, NC, NZ, NX = 4, 2, 8, 4
MESH = pl.DeviceIdType.MESH
f32 = jnp.float32
bf16 = jnp.bfloat16

TOP = 448.0
TINY = 1e-6
ROWS = 32
W = 512
HID = 448
PAIR = 2 * HID
R128 = 128 ** -0.5
R64 = 64 ** -0.5


def mm(a, b):
    return lax.dot_general(a, b, (((1,), (0,)), ((), ())), preferred_element_type=f32)


def mm_t(a, b):
    return lax.dot_general(a, b, (((1,), (1,)), ((), ())), preferred_element_type=f32)


def table(size, block):
    i = lax.broadcasted_iota(jnp.int32, (size, size), 0)
    j = lax.broadcasted_iota(jnp.int32, (size, size), 1)
    v = i & j & (block - 1)
    v = v ^ (v >> 4)
    v = v ^ (v >> 2)
    v = v ^ (v >> 1)
    sign = 1 - 2 * (v & 1)
    same = (i & ~(block - 1)) == (j & ~(block - 1))
    return jnp.where(same, sign, 0).astype(f32).astype(bf16)


def cut(n):
    at = 0
    while at < n:
        yield at, min(256, n - at)
        at += 256


def split(v, terms):
    parts = []
    for _ in range(terms):
        p = v.astype(bf16)
        parts.append(p)
        v = v - p.astype(f32)
    return parts


def turn_cols(v, h, terms=1):
    parts = split(v, terms) if terms > 1 else [v]
    outs = []
    for at, n in cut(v.shape[1]):
        outs.append(sum(mm(p[:, at : at + n], h[:n, :n]) for p in parts))
    return jnp.concatenate(outs, axis=1)


def encode(v, dst):
    hi = v.astype(bf16)
    dst[0:64] = hi
    hi = hi.astype(f32)
    unit = jnp.abs(hi) * (2.0**-8 / 7.0)
    n = jnp.where(unit > 0, (v - hi) / jnp.where(unit > 0, unit, 1.0), 0.0)
    n = jnp.clip(jnp.floor(n + 0.5), -7.0, 7.0) + 7.0
    dst[64:96] = (n[0:32] * 15.0 + n[32:64]).astype(bf16)


def decode(src):
    hi = src[0:64].astype(f32)
    code = src[64:96].astype(f32)
    first = jnp.floor((code + 0.5) * (1.0 / 15.0))
    n = jnp.concatenate([first, code - first * 15.0], axis=0) - 7.0
    return hi + n * (jnp.abs(hi) * (2.0**-8 / 7.0))


class Net:
    def __init__(self, send, recv):
        self.send_sems, self.recv_sems = send, recv
        self.n = 0
        self.all = []

    def send(self, src, dst, **dev):
        i = self.n
        self.n += 1
        names = {"y": "gx_0", "c": "gx_1", "z": "gy_0", "x": "gy_1"}
        d = pltpu.make_async_remote_copy(
            src_ref=src,
            dst_ref=dst,
            send_sem=self.send_sems.at[i],
            recv_sem=self.recv_sems.at[i],
            device_id={names[k]: v for k, v in dev.items()},
            device_id_type=MESH,
        )
        d.start()
        self.all.append(d)
        return d


class Peaks:
    def __init__(self, net, src, buf, me):
        self.net, self.src, self.buf = net, src, buf
        self.y, self.c, self.z, self.x = me

    def start(self, v):
        self.src[0] = v
        self.h = []
        for j in range(1, 8):
            dy, dc = j // 2, j % 2
            self.h.append(
                self.net.send(
                    self.src.at[0], self.buf.at[j - 1], y=(self.y + dy) % NY, c=(self.c + dc) % NC
                )
            )

    def gathered(self, level, at, n):
        for h in self.h:
            h.wait_recv()
        v = self.src[level]
        for j in range(n):
            v = jnp.maximum(v, self.buf[at + j])
        return v

    def second(self):
        self.src[1] = self.gathered(0, 0, 7)
        self.h = [
            self.net.send(self.src.at[1], self.buf.at[6 + j], x=(self.x + j) % NX)
            for j in range(1, NX)
        ]

    def third(self):
        self.src[2] = self.gathered(1, 7, 3)
        self.h = [
            self.net.send(self.src.at[2], self.buf.at[9 + j], z=(self.z + j) % NZ)
            for j in range(1, NZ)
        ]

    def result(self):
        return self.gathered(2, 10, 7)


N_SEMS = 220


def kernel(
    tok, cot, wg, wu, wd,
    out, ig, gg, ug, dg,
    h128, h64, t_all, c_all, tc, tct, rg, ru, rd, cg, cu, cd,
    pk_src, pk_buf, ph_src, ph_buf, pk, ph,
    dsrc, drecv, acc, ysrc, yrel, yfin, bsrc, brel, bfin,
    h_all, a_all, ch, cht, ga, ua,
    o_part, osrc, orel, ofin, ozs, ozr,
    i_part, isrc, irecv, ixs, ixr,
    ssem, rsem,
):
    y = lax.axis_index("gx_0")
    c = lax.axis_index("gx_1")
    z = lax.axis_index("gy_0")
    x = lax.axis_index("gy_1")
    pc = 1 - c
    net = Net(ssem, rsem)
    send = net.send
    yp, ym, y2 = (y + 1) % NY, (y + 3) % NY, (y + 2) % NY
    xp, xm, x2 = (x + 1) % NX, (x + 3) % NX, (x + 2) % NX
    zp, zm = (z + 1) % NZ, (z + 7) % NZ

    barrier = pltpu.get_barrier_semaphore()
    for j in range(1, 8):
        pl.semaphore_signal(
            barrier, inc=1, device_id={"gx_0": (y + j // 2) % NY, "gx_1": (c + j % 2) % NC},
            device_id_type=MESH,
        )
    for j in range(1, NX):
        pl.semaphore_signal(barrier, inc=1, device_id={"gy_1": (x + j) % NX}, device_id_type=MESH)
    for j in range(1, NZ):
        pl.semaphore_signal(barrier, inc=1, device_id={"gy_0": (z + j) % NZ}, device_id_type=MESH)
    h128[...] = table(256, 128)
    h64[...] = table(256, 64)
    t_all[z, x] = tok[...]
    c_all[z, x] = cot[...]
    pl.semaphore_wait(barrier, 7 + 3 + 7)

    def zat(d):
        return (z + d + NZ) % NZ

    xs = [(x + NX - j) % NX for j in range(NX)]
    tx, tzp, tzm = {}, {}, {}
    for j in range(1, NX):
        tx[j] = send(tok, t_all.at[z, x], x=(x + j) % NX)

    def t_step(s, j):
        if s < 3 or j < 2:
            b = zat(-s)
            src = tok if s == 0 and j == 0 else t_all.at[b, xs[j]]
            tzp[s, j] = send(src, t_all.at[b, xs[j]], z=zp)
        if s < 3 or j >= 2:
            b = zat(s)
            src = tok if s == 0 and j == 0 else t_all.at[b, xs[j]]
            tzm[s, j] = send(src, t_all.at[b, xs[j]], z=zm)

    def t_wait(s, j):
        if (s, j) in tzp:
            tzp[s, j].wait_recv()
        if (s, j) in tzm:
            tzm[s, j].wait_recv()

    czp, czm, cxp, cxm, crp, crm = {}, {}, {}, {}, {}, {}

    def c_step(s):
        if s < 3:
            bp, bm = zat(-s), zat(s)
            czp[s] = send(cot if s == 0 else c_all.at[bp, x], c_all.at[bp, x], z=zp)
            czm[s] = send(cot if s == 0 else c_all.at[bm, x], c_all.at[bm, x], z=zm)
        else:
            bp, bm = zat(-3), zat(3)
            lo = c_all.at[bp, x, pl.ds(0, 16)]
            hi = c_all.at[bm, x, pl.ds(16, 16)]
            czp[s] = send(lo, lo, z=zp)
            czm[s] = send(hi, hi, z=zm)

    def c_wait(s):
        czp[s].wait_recv()
        czm[s].wait_recv()

    def c_x(d):
        src = cot if d == 0 else c_all.at[zat(d), x]
        cxp[d] = send(src, c_all.at[zat(d), x], x=xp)
        cxm[d] = send(src, c_all.at[zat(d), x], x=xm)

    def c_relay(d):
        cxp[d].wait_recv()
        lo = c_all.at[zat(d), xm, pl.ds(0, 16)]
        crp[d] = send(lo, lo, x=xp)
        cxm[d].wait_recv()
        hi = c_all.at[zat(d), xp, pl.ds(16, 16)]
        crm[d] = send(hi, hi, x=xm)

    t_step(0, 0)
    c_step(0)
    c_x(0)

    p_x = jnp.max(jnp.abs(turn_cols(tok[...], h128))) * R128
    for at, n in cut(W):
        rg[at : at + n] = mm(h128[...], wg[at : at + n]) * R128
        ru[at : at + n] = mm(h128[...], wu[at : at + n]) * R128
    for at, n in cut(HID):
        rd[at : at + n] = mm(h64[:n, :n], wd[at : at + n]) * R64
    p_g = jnp.max(jnp.abs(rg[...]))
    p_u = jnp.max(jnp.abs(ru[...]))
    p_d = jnp.max(jnp.abs(rd[...]))
    row = lax.broadcasted_iota(jnp.int32, (8, 128), 0)
    peaks = Peaks(net, pk_src, pk_buf, (y, c, z, x))
    peaks.start(
        jnp.where(row == 0, p_x, jnp.where(row == 1, p_g, jnp.where(row == 2, p_u, p_d)))
    )
    for j in range(1, NX):
        tx[j].wait_recv()
        t_step(0, j)
    c_wait(0)
    c_step(1)
    c_x(1)
    c_x(-1)
    peaks.second()
    for j in range(NX):
        t_wait(0, j)
        t_step(1, j)
    c_wait(1)
    c_step(2)
    c_x(2)
    c_x(-2)
    c_relay(0)
    peaks.third()
    for j in range(NX):
        t_wait(1, j)
        t_step(2, j)
    c_wait(2)
    c_step(3)
    c_x(3)
    c_x(-3)
    c_relay(1)
    c_relay(-1)
    pk[...] = peaks.result()
    inv_x = 1.0 / (pk[0:1, 0:1] + TINY)
    cg[...] = (TOP * jnp.tanh(rg[...] * (1.0 / (pk[1:2, 0:1] + TINY)))).astype(bf16)
    cu[...] = (TOP * jnp.tanh(ru[...] * (1.0 / (pk[2:3, 0:1] + TINY)))).astype(bf16)
    cd[...] = (TOP * jnp.tanh(rd[...] * (1.0 / (pk[3:4, 0:1] + TINY)))).astype(bf16)
    for j in range(NX):
        t_wait(2, j)
        t_step(3, j)
    c_wait(3)
    c_x(4)
    c_relay(2)
    c_relay(-2)
    for j in range(NX):
        t_wait(3, j)
    c_relay(3)
    c_relay(-3)
    c_relay(4)

    def cast_tokens(k, carry):
        t = t_all[k].reshape(4 * ROWS, W)
        v = (TOP * jnp.tanh(turn_cols(t, h128) * R128 * inv_x)).astype(bf16)
        tc[k] = v
        tct[:, pl.ds(pl.multiple_of(k * 128, 128), 128)] = v.T
        return carry

    lax.fori_loop(0, 8, cast_tokens, 0)
    for d in (0, 1, -1, 2, -2, 3, -3, 4):
        crp[d].wait_recv()
        crm[d].wait_recv()

    def block(k, dst):
        t = tc[k]
        dst[0:128, 0:HID] = mm(t, cg[...]).astype(dst.dtype)
        dst[0:128, HID:PAIR] = mm(t, cu[...]).astype(dst.dtype)
        b = mm_t(c_all[k].reshape(4 * ROWS, W), cd[...]).astype(dst.dtype)
        dst[128:192, 0:HID] = b[0:64]
        dst[128:192, HID:PAIR] = b[64:128]

    order = [y2, yp, ym, y]
    dh = {}

    def both(i):
        block(order[i] * 2 + pc, dsrc.at[i])
        dh[i] = send(dsrc.at[i], drecv.at[i], c=pc)
        block(order[i] * 2 + c, acc.at[i])

    def q(i, at, n):
        return acc[i, at : at + n] + drecv[i, at : at + n]

    def put(slot, v, dst, **dev):
        encode(v, ysrc.at[slot])
        return send(ysrc.at[slot], dst, **dev)

    def put_h(slot, v, dst, **dev):
        bsrc[slot] = v.astype(bf16)
        return send(bsrc.at[slot], dst, **dev)

    both(0)
    both(1)
    dh[0].wait_recv()
    relp = put(0, q(0, 0, 64), yrel.at[0], y=yp)
    relm = put(1, q(0, 64, 64), yrel.at[1], y=ym)
    both(2)
    dh[1].wait_recv()
    fp_hi = put(2, q(1, 64, 64), yfin.at[0, 1], y=yp)
    dh[2].wait_recv()
    fm_lo = put(3, q(2, 0, 64), yfin.at[1, 0], y=ym)
    both(3)
    relp.wait_recv()
    fp_lo = put(4, q(1, 0, 64) + decode(yrel.at[0]), yfin.at[0, 0], y=yp)
    relm.wait_recv()
    fm_hi = put(5, q(2, 64, 64) + decode(yrel.at[1]), yfin.at[1, 1], y=ym)
    brp = put_h(0, q(0, 128, 32), brel.at[0], y=yp)
    brm = put_h(1, q(0, 160, 32), brel.at[1], y=ym)
    bp_hi = put_h(2, q(1, 160, 32), bfin.at[0, 1], y=yp)
    bm_lo = put_h(3, q(2, 128, 32), bfin.at[1, 0], y=ym)
    brp.wait_recv()
    bp_lo = put_h(4, q(1, 128, 32) + brel[0].astype(f32), bfin.at[0, 0], y=yp)
    brm.wait_recv()
    bm_hi = put_h(5, q(2, 160, 32) + brel[1].astype(f32), bfin.at[1, 1], y=ym)
    dh[3].wait_recv()
    for h in (fp_hi, fm_lo, fp_lo, fm_hi):
        h.wait_recv()
    for i in range(2):
        acc[3, 64 * i : 64 * i + 64] = (
            q(3, 64 * i, 64) + decode(yfin.at[0, i]) + decode(yfin.at[1, i])
        )

    p_x, p_g, p_u, p_d = (pk[i : i + 1, 0:1] for i in range(4))
    gate = acc[3, 0:128, 0:HID] * (p_x * p_g / (TOP * TOP))
    up = acc[3, 0:128, HID:PAIR] * (p_x * p_u / (TOP * TOP))
    s = jax.nn.sigmoid(gate)
    hid = (gate * s * up).astype(bf16)
    h_all[y, c, :, 0:HID] = hid[0:64]
    h_all[y, c, :, HID:PAIR] = hid[64:128]

    def gather(buf, half):
        own = buf.at[y, c]
        hs = {"own": send(own, own, c=pc)}
        hs["p"] = send(own, own, y=yp)
        hs["m"] = send(own, own, y=ym)
        return hs

    def gather_relay(buf, half, hs):
        hs["p"].wait_recv()
        lo = buf.at[ym, c, pl.ds(0, half)]
        hs["rp"] = send(lo, lo, y=yp)
        hs["m"].wait_recv()
        hi = buf.at[yp, c, pl.ds(half, half)]
        hs["rm"] = send(hi, hi, y=ym)
        hs["fp"] = send(buf.at[ym, c], buf.at[ym, c], c=pc)
        hs["fm"] = send(buf.at[yp, c], buf.at[yp, c], c=pc)

    def gather_last(buf, hs):
        hs["rp"].wait_recv()
        hs["rm"].wait_recv()
        hs["f2"] = send(buf.at[y2, c], buf.at[y2, c], c=pc)

    def gather_done(hs):
        for n in ("own", "fp", "fm", "f2"):
            hs[n].wait_recv()

    hh = gather(h_all, 32)
    hidp = Peaks(net, ph_src, ph_buf, (y, c, z, x))
    p_h = jnp.max(jnp.abs(turn_cols(hid, h64))) * R64
    hidp.start(jnp.full((8, 128), p_h, f32))

    for h in (bp_hi, bm_lo, bp_lo, bm_hi):
        h.wait_recv()
    b = q(3, 128, 64) + jnp.concatenate(
        [bfin[0, i].astype(f32) + bfin[1, i].astype(f32) for i in range(2)], axis=0
    )
    b = turn_cols(b * (p_d / TOP), h64, 3) * R64
    hg = jnp.concatenate([b[:, 0:HID], b[:, HID:PAIR]], axis=0)
    a_all[y, c, :, 0:HID] = (hg * up * s * (1.0 + gate * (1.0 - s))).astype(bf16)
    a_all[y, c, :, HID:PAIR] = (hg * gate * s).astype(bf16)
    ah = gather(a_all, 64)
    gather_relay(h_all, 32, hh)
    hidp.second()
    gather_last(h_all, hh)
    gather_relay(a_all, 64, ah)
    hidp.third()
    gather_done(hh)
    ph[...] = hidp.result()
    inv_h = 1.0 / (ph[0:1, 0:1] + TINY)

    def cast_hidden(k, carry):
        v = h_all[k // 2, k % 2]
        v = (TOP * jnp.tanh(turn_cols(v, h64) * R64 * inv_h)).astype(bf16)
        ch[k, 0:64] = v[:, 0:HID]
        ch[k, 64:128] = v[:, HID:PAIR]
        v = ch[k]
        cht[:, pl.ds(pl.multiple_of(k * 128, 128), 128)] = v.T
        o_part[k] = mm(v, cd[...]).reshape(NX, ROWS, W)
        return carry

    lax.fori_loop(0, 8, cast_hidden, 0)
    gather_last(a_all, ah)

    for d in range(NZ):
        osrc[0, d] = o_part[zat(d), x2].astype(bf16)
    L4, H4 = pl.ds(0, 4), pl.ds(4, 4)
    o_rp = send(osrc.at[0, L4], orel.at[0], x=xp)
    o_rm = send(osrc.at[0, H4], orel.at[1], x=xm)
    for d in range(4):
        osrc[1, 4 + d] = o_part[zat(4 + d), xp].astype(bf16)
        osrc[2, d] = o_part[zat(d), xm].astype(bf16)
    o_fph = send(osrc.at[1, H4], ofin.at[0, H4], x=xp)
    o_fml = send(osrc.at[2, L4], ofin.at[1, L4], x=xm)

    gather_done(ah)
    for k in range(8):
        ga[k] = a_all[k // 2, k % 2, :, 0:HID]
        ua[k] = a_all[k // 2, k % 2, :, HID:PAIR]

    def input_part(k):
        v = mm_t(ga[k], cg[...]) * (p_g / TOP) + mm_t(ua[k], cu[...]) * (p_u / TOP)
        i_part[k] = v.reshape(NX, ROWS, W)

    input_part(zat(4))
    isrc[0, 0] = i_part[zat(4)].astype(bf16)
    ip, im = {}, {}
    for j in range(NX):
        if j < 2:
            ip[0, j] = send(isrc.at[0, 0, j], irecv.at[0, 0, j], z=zp)
        else:
            im[0, j] = send(isrc.at[0, 0, j], irecv.at[1, 0, j], z=zm)

    o_rp.wait_recv()
    for d in range(4):
        osrc[1, d] = (o_part[zat(d), xp] + orel[0, d].astype(f32)).astype(bf16)
    o_fpl = send(osrc.at[1, L4], ofin.at[0, L4], x=xp)
    o_rm.wait_recv()
    for d in range(4):
        osrc[2, 4 + d] = (o_part[zat(4 + d), xm] + orel[1, d].astype(f32)).astype(bf16)
    o_fmh = send(osrc.at[2, H4], ofin.at[1, H4], x=xm)

    input_part(zat(3))
    input_part(zat(-3))

    def ring(s):
        for side, d, handles, dev in ((0, 4 - s, ip, zp), (1, s - 4, im, zm)):
            for j in (2, 3, 0, 1) if side == 0 else (0, 1, 2, 3):
                v = i_part[zat(d), j]
                if (s - 1, j) in handles:
                    handles[s - 1, j].wait_recv()
                    v = v + irecv[side, s - 1, j].astype(f32)
                isrc[side, s, j] = v.astype(bf16)
                handles[s, j] = send(isrc.at[side, s, j], irecv.at[side, s, j], z=dev)

    ring(1)
    input_part(zat(2))
    input_part(zat(-2))
    ring(2)
    input_part(zat(1))
    input_part(zat(-1))
    ring(3)
    input_part(z)

    for h in (o_fph, o_fml, o_fpl, o_fmh):
        h.wait_recv()
    oz = {}
    for d in range(NZ):
        v = o_part[zat(d), x] + ofin[0, d].astype(f32) + ofin[1, d].astype(f32)
        if d == 0:
            o_part[z, x] = v
        else:
            ozs[d] = v.astype(bf16)
            oz[d] = send(ozs.at[d], ozr.at[d], z=zat(d))

    for j in range(NX):
        ip[3, j].wait_recv()
        im[3, j].wait_recv()
        ixs[j] = (i_part[z, j] + irecv[0, 3, j].astype(f32) + irecv[1, 3, j].astype(f32)).astype(
            bf16
        )
    ix = {}
    for j in range(1, NX):
        ix[j] = send(ixs.at[(x + j) % NX], ixr.at[j], x=(x + j) % NX)

    p_h = ph[0:1, 0:1]

    def turn_rows(v, h, n):
        return sum(mm(h, p) for p in split(v, 2))

    for at, n in cut(HID):
        v = mm(cht[at : at + n], c_all[...].reshape(1024, W)) * (p_h / TOP)
        dg[at : at + n] = (turn_rows(v, h64[:n, :n], n) * R64).astype(bf16)
    for at, n in cut(W):
        for acts, dst in ((ga, gg), (ua, ug)):
            v = mm(tct[at : at + n], acts[...].reshape(1024, HID)) * (p_x / TOP)
            dst[at : at + n] = (turn_rows(v, h128[...], n) * R128).astype(bf16)

    v = o_part[z, x]
    for d in range(1, NZ):
        oz[d].wait_recv()
        v = v + ozr[d].astype(f32)
    out[...] = (v * (p_h * p_d / (TOP * TOP))).astype(bf16)

    v = i_part[z, x] + irecv[0, 3, x].astype(f32) + irecv[1, 3, x].astype(f32)
    for j in range(1, NX):
        ix[j].wait_recv()
        v = v + ixr[j].astype(f32)
    ig[...] = (turn_cols(v, h128, 3) * R128).astype(bf16)

    for h in net.all:
        h.wait_send()


def shards(tokens, cotangent, gate_weight, up_weight, down_weight):
    def vm(shape, dtype):
        return pltpu.VMEM(shape, dtype)

    scratch = [
        vm((256, 256), bf16), vm((256, 256), bf16),
        vm((NZ, NX, ROWS, W), bf16), vm((NZ, NX, ROWS, W), bf16),
        vm((8, 128, W), bf16), vm((W, 1024), bf16),
        vm((W, HID), f32), vm((W, HID), f32), vm((HID, W), f32),
        vm((W, HID), bf16), vm((W, HID), bf16), vm((HID, W), bf16),
        vm((3, 8, 128), f32), vm((17, 8, 128), f32), vm((3, 8, 128), f32), vm((17, 8, 128), f32),
        vm((8, 128), f32), vm((8, 128), f32),
        vm((4, 192, PAIR), f32), vm((4, 192, PAIR), f32), vm((4, 192, PAIR), f32),
        vm((6, 96, PAIR), bf16), vm((2, 96, PAIR), bf16), vm((2, 2, 96, PAIR), bf16),
        vm((6, 32, PAIR), bf16), vm((2, 32, PAIR), bf16), vm((2, 2, 32, PAIR), bf16),
        vm((NY, NC, 64, PAIR), bf16), vm((NY, NC, 128, PAIR), bf16),
        vm((8, 128, HID), bf16), vm((HID, 1024), bf16), vm((8, 128, HID), bf16), vm((8, 128, HID), bf16),
        vm((NZ, NX, ROWS, W), f32), vm((3, NZ, ROWS, W), bf16), vm((2, 4, ROWS, W), bf16),
        vm((2, NZ, ROWS, W), bf16), vm((NZ, ROWS, W), bf16), vm((NZ, ROWS, W), bf16),
        vm((NZ, NX, ROWS, W), f32), vm((2, 4, NX, ROWS, W), bf16), vm((2, 4, NX, ROWS, W), bf16),
        vm((NX, ROWS, W), bf16), vm((NX, ROWS, W), bf16),
        pltpu.SemaphoreType.DMA((N_SEMS,)), pltpu.SemaphoreType.DMA((N_SEMS,)),
    ]
    vmem = pl.BlockSpec(memory_space=pltpu.VMEM)
    return pl.pallas_call(
        kernel,
        out_shape=[
            jax.ShapeDtypeStruct((ROWS, W), bf16),
            jax.ShapeDtypeStruct((ROWS, W), bf16),
            jax.ShapeDtypeStruct((W, HID), bf16),
            jax.ShapeDtypeStruct((W, HID), bf16),
            jax.ShapeDtypeStruct((HID, W), bf16),
        ],
        in_specs=[vmem] * 5,
        out_specs=[vmem] * 5,
        scratch_shapes=scratch,
        compiler_params=pltpu.CompilerParams(
            collective_id=0, has_side_effects=True, vmem_limit_bytes=60 * 1024 * 1024
        ),
    )(tokens, cotangent, gate_weight, up_weight, down_weight)


def solution(mesh):
    fine = Mesh(mesh.devices.reshape(NY, NC, NZ, NX), GX + GY)
    specs = (P(GY, GX), P(GY, GX), P(GX, GY), P(GX, GY), P(GY, GX))
    return jax.shard_map(
        shards, mesh=fine, in_specs=specs, out_specs=specs, check_vma=False
    )
```

time: 337 us -> 113 us (0.34)
  the two profiles are of different devices: /device:TPU:16 before, /device:TPU:64 now
where the time goes in v1:
time: 113 us; the launch traced here: 112 us
  Pallas kernels  103 us (91%)
  local copies, waits for them, and re-layouts  8.26 us (7%)
    pallas_call x1, Pallas kernels, shards(): pl.pallas_call(kernel, out_shape=[jax.ShapeDtypeStruct((ROWS, W), bf16),...  103 us
    unnamed x15, local copies, waits for them, and re-layouts  5.23 us
    pallas_call x2, local copies, waits for them, and re-layouts, shards(): pl.pallas_call(kernel, out_shape=[jax.ShapeDtypeStruct((ROWS, W), bf16),...  3.02 us

profile of v1, /device:TPU:64, one launch (start us, length us, event | category | flops | bytes accessed | tf_op | source)
XLA Modules:
  0.0 112.3 jit_solution(16310309171035804267)
XLA Ops:
  0.6 0.0 copy-start.2
  0.6 2.1 %copy.10.wg = bf16[512,448]{1,0:T(8,128)(2,1)} copy(bf16[512,448]{0,1:T(8,128)(2,1)} %param.7) | data formatting | bytes 917504 | tf_op args[2]
  2.7 0.0 copy-done.2
  2.7 1.0 copy.11.wu
  3.7 103.4 %shard_map.92 = (bf16[32,512]{1,0:T(8,128)(2,1)}, bf16[32,512]{1,0:T(8,128)(2,1)}, bf16[512,448]{1,0:T(8,128)(2,1)}, bf16[512,448]{1,0:T(8,128)(2,1)}, bf16[448,512]{1,0:T(8,128)(2,1)}) custom-call(bf16[32,512]{1,0:T(8,128)(2,1)} %tok.1, bf16[32,512]{1,0:T(8,128)(2,1)} %cot.1, bf16[512,448]{1,0:T(8,128)(2,1)} %copy.10.wg, bf16[512,448]{1,0:T(8,128)(2,1)} %copy.11.wu, ...), custom_call_target="tpu_custom_call" | custom-call | tf_op jit(solution)/shard_map/pallas_call | solution.py:588
  107.1 0.0 copy-start
  107.2 2.1 %copy.12 = bf16[512,448]{0,1:T(8,128)(2,1)} copy(bf16[512,448]{1,0:T(8,128)(2,1)} %get-tuple-element.7) | data formatting | bytes 917504 | tf_op jit(solution)/shard_map/pallas_call | solution.py:588
  109.2 0.0 copy-done
  109.2 0.0 copy-start.4
  109.2 0.0 copy-start.1
  109.2 1.0 copy.13
  110.2 0.0 copy-done.4
  110.2 0.0 copy-start.3
  110.2 0.6 copy.17
  110.8 0.2 copy-done.3
  111.0 0.6 copy.18
  111.6 0.0 copy-done.1
  111.6 0.8 copy.19
Async XLA Ops:
  0.6 2.1 %copy-start.2 = (bf16[512,448]{0,1:T(8,128)(2,1)S(1)}, bf16[512,448]{0,1:T(8,128)(2,1)}, u32[]{:S(2)}) copy-start(bf16[512,448]{0,1:T(8,128)(2,1)} %param.8) | copy-start | bytes 1376260
  107.1 2.1 %copy-start = (bf16[512,448]{1,0:T(8,128)(2,1)S(1)}, bf16[512,448]{1,0:T(8,128)(2,1)}, u32[]{:S(2)}) copy-start(bf16[512,448]{1,0:T(8,128)(2,1)} %get-tuple-element.8) | copy-start | bytes 1376260
  109.2 1.0 copy-start.4
  109.2 2.4 %copy-start.1 = (bf16[448,512]{1,0:T(8,128)(2,1)S(1)}, bf16[448,512]{1,0:T(8,128)(2,1)}, u32[]{:S(2)}) copy-start(bf16[448,512]{1,0:T(8,128)(2,1)} %get-tuple-element.19) | copy-start | bytes 1376260
  110.2 0.8 copy-start.3

commit v2 on v1

v2 whole, which is shorter than its diff:
```python
import functools

import jax
import jax.numpy as jnp
from jax import lax
from jax.experimental import pallas as pl
from jax.experimental.pallas import tpu as pltpu
from jax.sharding import Mesh
from jax.sharding import PartitionSpec as P

GY = ("gy_0", "gy_1")
GX = ("gx_0", "gx_1")
NY, NC, NZ, NX = 4, 2, 8, 4
MESH = pl.DeviceIdType.MESH
f32 = jnp.float32
bf16 = jnp.bfloat16

TOP = 448.0
TINY = 1e-6
ROWS = 32
W = 512
HID = 448
PAIR = 2 * HID
R128 = 128 ** -0.5
R64 = 64 ** -0.5


def mm(a, b):
    return lax.dot_general(a, b, (((1,), (0,)), ((), ())), preferred_element_type=f32)


def mm_t(a, b):
    return lax.dot_general(a, b, (((1,), (1,)), ((), ())), preferred_element_type=f32)


def table(size, block):
    i = lax.broadcasted_iota(jnp.int32, (size, size), 0)
    j = lax.broadcasted_iota(jnp.int32, (size, size), 1)
    v = i & j & (block - 1)
    v = v ^ (v >> 4)
    v = v ^ (v >> 2)
    v = v ^ (v >> 1)
    sign = 1 - 2 * (v & 1)
    same = (i & ~(block - 1)) == (j & ~(block - 1))
    return jnp.where(same, sign, 0).astype(f32).astype(bf16)


def cut(n):
    at = 0
    while at < n:
        yield at, min(256, n - at)
        at += 256


def split(v, terms):
    parts = []
    for _ in range(terms):
        p = v.astype(bf16)
        parts.append(p)
        v = v - p.astype(f32)
    return parts


def turn_cols(v, h, terms=1):
    parts = split(v, terms) if terms > 1 else [v]
    outs = []
    for at, n in cut(v.shape[1]):
        outs.append(sum(mm(p[:, at : at + n], h[:n, :n]) for p in parts))
    return jnp.concatenate(outs, axis=1)


def encode(v, dst):
    hi = v.astype(bf16)
    dst[0:64] = hi
    hi = hi.astype(f32)
    unit = jnp.abs(hi) * (2.0**-8 / 7.0)
    n = jnp.where(unit > 0, (v - hi) / jnp.where(unit > 0, unit, 1.0), 0.0)
    n = jnp.clip(jnp.floor(n + 0.5), -7.0, 7.0) + 7.0
    dst[64:96] = (n[0:32] * 15.0 + n[32:64]).astype(bf16)


def decode(src):
    hi = src[0:64].astype(f32)
    code = src[64:96].astype(f32)
    first = jnp.floor((code + 0.5) * (1.0 / 15.0))
    n = jnp.concatenate([first, code - first * 15.0], axis=0) - 7.0
    return hi + n * (jnp.abs(hi) * (2.0**-8 / 7.0))


class Net:
    def __init__(self, send, recv):
        self.send_sems, self.recv_sems = send, recv
        self.n = self.phase = 0
        self.sent = [0] * N_PHASES

    def sem(self):
        self.n += 1
        return self.n - 1

    def copy(self, src, dst, sem, **dev):
        names = {"y": "gx_0", "c": "gx_1", "z": "gy_0", "x": "gy_1"}
        return pltpu.make_async_remote_copy(
            src_ref=src,
            dst_ref=dst,
            send_sem=self.send_sems.at[self.phase],
            recv_sem=self.recv_sems.at[sem],
            device_id={names[k]: v for k, v in dev.items()},
            device_id_type=MESH,
        )

    def count(self, src, copies=1):
        size = copies * src.dtype.itemsize
        for n in src.shape:
            size *= n
        self.sent[self.phase] += size

    def send(self, src, dst, sem=None, **dev):
        d = self.copy(src, dst, self.sem() if sem is None else sem, **dev)
        d.start()
        self.count(src)
        return d

    def wait(self, sem, ref):
        self.copy(ref, ref, sem, c=1 - lax.axis_index("gx_1")).wait_recv()

    def wait_sent(self, ref):
        for self.phase in range(N_PHASES):
            part = ref.at[pl.ds(0, self.sent[self.phase] // 4096)]
            self.copy(part, part, 0, c=1 - lax.axis_index("gx_1")).wait_send()


class Peaks:
    def __init__(self, net, src, buf, me):
        self.net, self.src, self.buf = net, src, buf
        self.y, self.c, self.z, self.x = me

    def start(self, v):
        self.src[0] = v
        self.sem = self.net.sem()
        for j in range(1, 8):
            dy, dc = j // 2, j % 2
            self.net.send(
                self.src.at[0], self.buf.at[j - 1], self.sem, y=(self.y + dy) % NY, c=(self.c + dc) % NC
            )

    def gathered(self, level, at, n):
        self.net.wait(self.sem, self.buf.at[pl.ds(at, n)])
        v = self.src[level]
        for j in range(n):
            v = jnp.maximum(v, self.buf[at + j])
        return v

    def second(self):
        self.src[1] = self.gathered(0, 0, 7)
        self.sem = self.net.sem()
        for j in range(1, NX):
            self.net.send(self.src.at[1], self.buf.at[6 + j], self.sem, x=(self.x + j) % NX)

    def third(self):
        self.src[2] = self.gathered(1, 7, 3)
        self.sem = self.net.sem()
        for j in range(1, NZ):
            self.net.send(self.src.at[2], self.buf.at[9 + j], self.sem, z=(self.z + j) % NZ)

    def result(self):
        return self.gathered(2, 10, 7)


class ZX:
    def __init__(self, net, own, buf, z, x):
        self.net, self.own, self.buf, self.z, self.x = net, own, buf, z, x
        self.came, self.crossed = {}, {}
        self.relays = net.sem()

    def at(self, d):
        return (self.z + d + NZ) % NZ

    def start(self):
        for d in (1, -1, 2, -2, 3, -3, 4):
            h = self.net.send(self.own, self.buf.at[self.z, self.x], z=self.at(d))
            self.came[4 if d == 4 else -d] = h

    def cross(self, d):
        b = self.at(d)
        src = self.own
        if d:
            self.came[d].wait_recv()
            src = self.buf.at[b, self.x]
        self.crossed[d] = self.net.sem()
        for k in (1, 3):
            self.net.send(src, self.buf.at[b, self.x], self.crossed[d], x=(self.x + k) % NX)

    def relay(self, d):
        b, xp, xm = self.at(d), (self.x + 1) % NX, (self.x + 3) % NX
        self.net.wait(self.crossed[d], self.buf.at[0, pl.ds(0, 2)])
        lo = self.buf.at[b, xm, pl.ds(0, 16)]
        self.net.send(lo, lo, self.relays, x=xp)
        hi = self.buf.at[b, xp, pl.ds(16, 16)]
        self.net.send(hi, hi, self.relays, x=xm)

    def done(self):
        self.net.wait(self.relays, self.buf.at[pl.ds(0, 2)])


class Gather:
    def __init__(self, net, buf, half, y, c, together):
        self.net, self.buf, self.half, self.y, self.c = net, buf, half, y, c
        self.yp, self.ym, self.y2 = (y + 1) % NY, (y + 3) % NY, (y + 2) % NY
        self.pair = net.sem() if together else None
        self.rest = net.sem()

    def part(self, y, i):
        return self.buf.at[y, self.c, pl.ds(i * self.half, self.half)]

    def to_pair(self, y):
        return self.net.send(self.buf.at[y, self.c], self.buf.at[y, self.c], self.pair, c=1 - self.c)

    def start(self):
        send, y = self.net.send, self.y
        self.p0 = send(self.part(y, 0), self.part(y, 0), y=self.yp)
        self.m1 = send(self.part(y, 1), self.part(y, 1), y=self.ym)
        self.p1 = send(self.part(y, 1), self.part(y, 1), y=self.yp)
        self.m0 = send(self.part(y, 0), self.part(y, 0), y=self.ym)
        self.own = self.to_pair(y)

    def relay(self):
        send = self.net.send
        self.p0.wait_recv()
        send(self.part(self.ym, 0), self.part(self.ym, 0), self.rest, y=self.yp)
        self.m1.wait_recv()
        send(self.part(self.yp, 1), self.part(self.yp, 1), self.rest, y=self.ym)

    def share(self):
        self.p1.wait_recv()
        self.fp = self.to_pair(self.ym)
        self.m0.wait_recv()
        self.fm = self.to_pair(self.yp)

    def last(self):
        self.net.wait(self.rest, self.buf.at[0, 0])
        self.f2 = self.to_pair(self.y2)

    def done(self):
        self.net.wait(self.pair, self.buf.at[:, 0])


N_SEMS = 110
N_PHASES = 5
MOST_SENT = 1280
RELATIVE = (4, 3, -3, 2, -2, 1, -1, 0)


def kernel(
    tok, cot, wg_hbm, wu_hbm, wd_hbm,
    gg_hbm, ug_hbm, dg_hbm, out_hbm, ig_hbm,
    h128, h64, wts, t_all, c_all, tc, rg, ru, rd, cg, cu, cd,
    pk_src, pk_buf, ph_src, ph_buf, pk, ph,
    dsrc, drecv, acc, ysrc, yrel, yfin, esrc, erecv, eacc, bsrc, brel, bfin,
    h_all, a_all, hrot, cht, gat, uat,
    o_part, osrc, orecv, oxs, oxr,
    i_part, isrc, irel, ifin, izf, izs, izr,
    small, grads, unread,
    ssem, rsem, lsem,
):
    y = lax.axis_index("gx_0")
    c = lax.axis_index("gx_1")
    z = lax.axis_index("gy_0")
    x = lax.axis_index("gy_1")
    pc = 1 - c
    net = Net(ssem, rsem)
    send = net.send
    yp, ym, y2 = (y + 1) % NY, (y + 3) % NY, (y + 2) % NY
    xp, xm, x2 = (x + 1) % NX, (x + 3) % NX, (x + 2) % NX
    zp, zm = (z + 1) % NZ, (z + 7) % NZ

    def zat(d):
        return (z + d + NZ) % NZ

    barrier = pltpu.get_barrier_semaphore()
    for j in range(1, 8):
        pl.semaphore_signal(
            barrier, inc=1, device_id={"gx_0": (y + j // 2) % NY, "gx_1": (c + j % 2) % NC},
            device_id_type=MESH,
        )
    for j in range(1, NX):
        pl.semaphore_signal(barrier, inc=1, device_id={"gy_1": (x + j) % NX}, device_id_type=MESH)
    for j in range(1, NZ):
        pl.semaphore_signal(barrier, inc=1, device_id={"gy_0": (z + j) % NZ}, device_id_type=MESH)
    loads = [
        pltpu.make_async_copy(w, wts.at[i], lsem.at[i]) for i, w in enumerate((wg_hbm, wu_hbm, wd_hbm))
    ]
    for load in loads:
        load.start()
    h128[...] = table(256, 128)
    h64[...] = table(256, 64)
    t_all[z, x] = tok[...]
    c_all[z, x] = cot[...]
    for load in loads:
        load.wait()

    def rotate_weights():
        rg[...] = turn_cols(wts[0], h128) * R128
        ru[...] = turn_cols(wts[1], h128) * R128
        for at, n in cut(HID):
            rd[at : at + n] = mm(h64[:n, :n], wts[2, at : at + n]) * R64

    p_x = jnp.max(jnp.abs(turn_cols(tok[...], h128))) * R128
    rotate_weights()
    p_g = jnp.max(jnp.abs(rg[...]))
    p_u = jnp.max(jnp.abs(ru[...]))
    p_d = jnp.max(jnp.abs(rd[...]))
    row = lax.broadcasted_iota(jnp.int32, (8, 128), 0)
    own_peaks = jnp.where(row == 0, p_x, jnp.where(row == 1, p_g, jnp.where(row == 2, p_u, p_d)))
    pl.semaphore_wait(barrier, 7 + 3 + 7)

    T = ZX(net, tok, t_all, z, x)
    C = ZX(net, cot, c_all, z, x)
    peaks = Peaks(net, pk_src, pk_buf, (y, c, z, x))
    T.start()
    peaks.start(own_peaks)
    T.cross(0)
    T.cross(1)
    T.cross(-1)
    T.relay(0)
    peaks.second()
    T.cross(2)
    T.cross(-2)
    T.relay(1)
    T.relay(-1)
    peaks.third()
    net.phase = 1
    C.start()
    T.cross(3)
    T.cross(-3)
    T.relay(2)
    T.relay(-2)
    T.cross(4)
    T.relay(3)
    T.relay(-3)
    C.cross(0)
    pk[...] = peaks.result()
    inv_x = 1.0 / (pk[0:1, 0:1] + TINY)
    cg[...] = (TOP * jnp.tanh(rg[...] * (1.0 / (pk[1:2, 0:1] + TINY)))).astype(bf16)
    cu[...] = (TOP * jnp.tanh(ru[...] * (1.0 / (pk[2:3, 0:1] + TINY)))).astype(bf16)
    T.relay(4)
    T.done()
    C.cross(1)
    C.cross(-1)
    C.relay(0)

    def gate_up(k, dst):
        t = turn_cols(t_all[k].reshape(4 * ROWS, W), h128)
        t = (TOP * jnp.tanh(t * (R128 * inv_x))).astype(bf16)
        tc[k] = t
        dst[:, 0:HID] = mm_t(t, cg[...])
        dst[:, HID:PAIR] = mm_t(t, cu[...])

    order = [y2, yp, ym, y]
    dh, eh = {}, {}

    def both(i):
        gate_up(order[i] * 2 + pc, dsrc.at[i])
        dh[i] = send(dsrc.at[i], drecv.at[i], c=pc)
        gate_up(order[i] * 2 + c, acc.at[i])

    def q(i, at):
        return acc[i, at : at + 64] + drecv[i, at : at + 64]

    def put(slot, v, dst, sem=None, **dev):
        encode(v, ysrc.at[slot])
        return send(ysrc.at[slot], dst, sem, **dev)

    net.phase = 2
    y_fin, b_fin = net.sem(), net.sem()
    both(0)
    both(1)
    dh[0].wait_recv()
    relp = put(0, q(0, 0), yrel.at[0], y=yp)
    relm = put(1, q(0, 64), yrel.at[1], y=ym)
    both(2)
    dh[1].wait_recv()
    put(2, q(1, 64), yfin.at[0, 1], y_fin, y=yp)
    dh[2].wait_recv()
    put(3, q(2, 0), yfin.at[1, 0], y_fin, y=ym)
    C.cross(2)
    C.cross(-2)
    C.relay(1)
    C.relay(-1)
    cd[...] = (TOP * jnp.tanh(rd[...] * (1.0 / (pk[3:4, 0:1] + TINY)))).astype(bf16)
    C.cross(3)
    C.cross(-3)
    C.relay(2)
    C.relay(-2)
    C.cross(4)
    relp.wait_recv()
    put(4, q(1, 0) + decode(yrel.at[0]), yfin.at[0, 0], y_fin, y=yp)
    relm.wait_recv()
    put(5, q(2, 64) + decode(yrel.at[1]), yfin.at[1, 1], y_fin, y=ym)
    both(3)
    C.relay(3)
    C.relay(-3)
    C.relay(4)
    C.done()

    def back(k, dst):
        b = mm_t(c_all[k].reshape(4 * ROWS, W), cd[...])
        dst[:, 0:HID] = b[0:64]
        dst[:, HID:PAIR] = b[64:128]

    def both_back(i):
        back(order[i] * 2 + pc, esrc.at[i])
        eh[i] = send(esrc.at[i], erecv.at[i], c=pc)
        back(order[i] * 2 + c, eacc.at[i])

    def e(i, at):
        return eacc[i, at : at + 32] + erecv[i, at : at + 32]

    def put_b(slot, v, dst, sem=None, **dev):
        bsrc[slot] = v.astype(bf16)
        return send(bsrc.at[slot], dst, sem, **dev)

    both_back(0)
    both_back(1)
    eh[0].wait_recv()
    brp = put_b(0, e(0, 0), brel.at[0], y=yp)
    brm = put_b(1, e(0, 32), brel.at[1], y=ym)
    both_back(2)
    eh[1].wait_recv()
    put_b(2, e(1, 32), bfin.at[0, 1], b_fin, y=yp)
    eh[2].wait_recv()
    put_b(3, e(2, 0), bfin.at[1, 0], b_fin, y=ym)
    both_back(3)

    dh[3].wait_recv()
    net.wait(y_fin, yfin)
    for i in range(2):
        acc[3, 64 * i : 64 * i + 64] = q(3, 64 * i) + decode(yfin.at[0, i]) + decode(yfin.at[1, i])
    p_x, p_g, p_u, p_d = (pk[i : i + 1, 0:1] for i in range(4))
    gate = acc[3, :, 0:HID] * (p_x * p_g / (TOP * TOP))
    up = acc[3, :, HID:PAIR] * (p_x * p_u / (TOP * TOP))
    s = jax.nn.sigmoid(gate)
    hid = (gate * s * up).astype(bf16)
    h_all[y, c, :, 0:HID] = hid[0:64]
    h_all[y, c, :, HID:PAIR] = hid[64:128]
    hidp = Peaks(net, ph_src, ph_buf, (y, c, z, x))
    p_h = jnp.max(jnp.abs(turn_cols(hid, h64))) * R64
    hidp.start(jnp.full((8, 128), p_h, f32))
    net.phase = 3
    H = Gather(net, h_all, 32, y, c, True)
    H.start()
    brp.wait_recv()
    put_b(4, e(1, 0) + brel[0].astype(f32), bfin.at[0, 0], b_fin, y=yp)
    brm.wait_recv()
    put_b(5, e(2, 32) + brel[1].astype(f32), bfin.at[1, 1], b_fin, y=ym)
    hidp.second()
    H.relay()
    eh[3].wait_recv()
    net.wait(b_fin, bfin)
    b = jnp.concatenate(
        [e(3, 32 * i) + bfin[0, i].astype(f32) + bfin[1, i].astype(f32) for i in range(2)], axis=0
    )
    b = turn_cols(b * (p_d / TOP), h64, 3) * R64
    hg = jnp.concatenate([b[:, 0:HID], b[:, HID:PAIR]], axis=0)
    a_all[y, c, :, 0:HID] = (hg * up * s * (1.0 + gate * (1.0 - s))).astype(bf16)
    a_all[y, c, :, HID:PAIR] = (hg * gate * s).astype(bf16)
    G = Gather(net, a_all, 64, y, c, False)
    G.start()
    hidp.third()
    H.share()
    H.last()
    H.done()

    def turn_hidden(k, carry):
        hrot[k] = turn_cols(h_all[k // 2, k % 2], h64) * R64
        return carry

    lax.fori_loop(0, 8, turn_hidden, 0)
    ph[...] = hidp.result()
    p_h = ph[0:1, 0:1]
    inv_h = 1.0 / (p_h + TINY)

    def o_block(d):
        k = zat(d)
        v = (TOP * jnp.tanh(hrot[k] * inv_h)).astype(bf16)
        v = jnp.concatenate([v[:, 0:HID], v[:, HID:PAIR]], axis=0)
        cht[:, pl.ds(pl.multiple_of(k * 128, 128), 128)] = v.T
        o_part[RELATIVE.index(d)] = mm(v, cd[...]).reshape(NX, ROWS, W)

    op, om = {}, {}
    o_last, o_cross = net.sem(), net.sem()

    def o_ring(s):
        for side, d, handles, dev in ((0, 4 - s, op, zp), (1, s - 4, om, zm)):
            i = RELATIVE.index(4 if s == 0 else d)
            for j in (2, 3, 0, 1) if side == 0 else (0, 1, 2, 3):
                if s == 0 and (j < 2) != (side == 0):
                    continue
                v = o_part[i, j]
                if (s - 1, j) in handles:
                    handles[s - 1, j].wait_recv()
                    v = v + orecv[side, s - 1, j].astype(f32)
                osrc[side, s, j] = v.astype(bf16)
                sem = o_last if s == 3 else None
                handles[s, j] = send(osrc.at[side, s, j], orecv.at[side, s, j], sem, z=dev)

    blocks = [(y, c), (y, pc), (ym, c), (yp, c), (ym, pc), (yp, pc), (y2, c), (y2, pc)]
    ir = {}
    i_fin = [net.sem() for _ in range(8)]
    i_owner = net.sem()

    def i_block(n):
        yy, cc = blocks[n]
        g = a_all[yy, cc, :, 0:HID]
        u = a_all[yy, cc, :, HID:PAIR]
        v = mm(g, cg[...]) * (p_g / TOP) + mm(u, cu[...]) * (p_u / TOP)
        i_part[n] = v.reshape(NX, ROWS, W)
        isrc[n, 0] = i_part[n, x2].astype(bf16)
        if n % 2 == 0:
            ir[n] = send(isrc.at[n, 0], irel.at[n], x=xp)
            isrc[n, 2] = i_part[n, xm].astype(bf16)
            send(isrc.at[n, 2], ifin.at[n, 1], i_fin[n], x=xm)
        else:
            ir[n] = send(isrc.at[n, 0], irel.at[n], x=xm)
            isrc[n, 1] = i_part[n, xp].astype(bf16)
            send(isrc.at[n, 1], ifin.at[n, 0], i_fin[n], x=xp)
        lanes = pl.ds(pl.multiple_of((yy * 2 + cc) * 128, 128), 128)
        gat[:, lanes] = g.T
        uat[:, lanes] = u.T

    def i_relay(n):
        ir[n].wait_recv()
        if n % 2 == 0:
            isrc[n, 1] = (i_part[n, xp] + irel[n].astype(f32)).astype(bf16)
            send(isrc.at[n, 1], ifin.at[n, 0], i_fin[n], x=xp)
        else:
            isrc[n, 2] = (i_part[n, xm] + irel[n].astype(f32)).astype(bf16)
            send(isrc.at[n, 2], ifin.at[n, 1], i_fin[n], x=xm)

    def i_final(n):
        yy, cc = blocks[n]
        net.wait(i_fin[n], ifin.at[n])
        k = yy * 2 + cc
        d = (k + NZ - z) % NZ
        v = i_part[n, x] + ifin[n, 0].astype(f32) + ifin[n, 1].astype(f32)
        izf[d] = v
        izs[d] = v.astype(bf16)

        @pl.when(d != 0)
        def _():
            net.copy(izs.at[d], izr.at[d], i_owner, z=k).start()

    net.phase = 4
    o_block(4)
    o_ring(0)
    G.relay()
    i_block(0)
    G.own.wait_recv()
    i_block(1)
    G.share()
    o_block(3)
    o_block(-3)
    o_ring(1)
    i_block(2)
    i_block(3)
    i_relay(0)
    i_relay(1)
    o_block(2)
    o_block(-2)
    G.last()
    o_ring(2)
    i_final(0)
    i_final(1)
    G.fp.wait_recv()
    i_block(4)
    G.fm.wait_recv()
    i_block(5)
    i_relay(2)
    i_relay(3)
    o_block(1)
    o_block(-1)
    i_block(6)
    G.f2.wait_recv()
    i_block(7)
    o_ring(3)
    i_final(2)
    i_final(3)
    i_relay(4)
    i_relay(5)
    o_block(0)
    i_relay(6)
    i_relay(7)
    i_final(4)
    i_final(5)

    stores = []

    def store(src, dst):
        copy = pltpu.make_async_copy(src, dst, lsem.at[3 + len(stores)])
        copy.start()
        stores.append(copy)

    for at, n in cut(HID):
        v = mm(cht[at : at + n], c_all[...].reshape(1024, W)) * (p_h / TOP)
        grads[2, at : at + n] = (sum(mm(h64[:n, :n], p) for p in split(v, 2)) * R64).astype(bf16)
    store(grads.at[2], dg_hbm)
    net.wait(o_last, orecv.at[:, 3])
    for j in range(NX):
        o_part[7, j] = o_part[7, j] + orecv[0, 3, j].astype(f32) + orecv[1, 3, j].astype(f32)
        oxs[j] = o_part[7, j].astype(bf16)
    for j in range(1, NX):
        send(oxs.at[(x + j) % NX], oxr.at[j], o_cross, x=(x + j) % NX)
    i_final(6)
    i_final(7)
    for i, (acts, dst) in enumerate(((gat, gg_hbm), (uat, ug_hbm))):
        for at, n in cut(HID):
            v = mm(acts[at : at + n], tc[...].reshape(1024, W)) * (p_x / TOP)
            grads[i, at : at + n] = (turn_cols(v, h128, 2) * R128).astype(bf16)
        store(grads.at[i], dst)
    v = o_part[7, x]
    net.wait(o_cross, oxr.at[pl.ds(1, NX - 1)])
    for j in range(1, NX):
        v = v + oxr[j].astype(f32)
    small[0] = (v * (p_h * p_d / (TOP * TOP))).astype(bf16)
    store(small.at[0], out_hbm)
    v = izf[0]
    net.count(izs.at[0], NZ - 1)
    net.wait(i_owner, izr.at[pl.ds(1, NZ - 1)])
    for d in range(1, NZ):
        v = v + izr[d].astype(f32)
    small[1] = (turn_cols(v, h128, 3) * R128).astype(bf16)
    store(small.at[1], ig_hbm)
    net.wait_sent(unread)
    for copy in stores:
        copy.wait()


def hand_over(*refs):
    n = len(refs) // 3
    given, sems = refs[: 2 * n], refs[-1]
    kept = refs[2 * n : 3 * n]
    copies = []
    for i in range(n):
        copies.append(pltpu.make_async_copy(given[i], kept[i], sems.at[i]))
        copies[i].start()
    outs = []
    for i in range(n):
        copies[i].wait()
        outs.append(pltpu.make_async_copy(kept[i], given[n + i], sems.at[n + i]))
        outs[i].start()
    for out in outs:
        out.wait()


def shards(tokens, cotangent, gate_weight, up_weight, down_weight):
    def vm(shape, dtype):
        return pltpu.VMEM(shape, dtype)

    part = (NZ, NX, ROWS, W)
    scratch = [
        vm((256, 256), bf16), vm((256, 256), bf16), vm((3, HID, W), bf16),
        vm(part, bf16), vm(part, bf16), vm((8, 128, W), bf16),
        vm((HID, W), f32), vm((HID, W), f32), vm((HID, W), f32),
        vm((HID, W), bf16), vm((HID, W), bf16), vm((HID, W), bf16),
        vm((3, 8, 128), f32), vm((17, 8, 128), f32), vm((3, 8, 128), f32), vm((17, 8, 128), f32),
        vm((8, 128), f32), vm((8, 128), f32),
        vm((4, 128, PAIR), f32), vm((4, 128, PAIR), f32), vm((4, 128, PAIR), f32),
        vm((6, 96, PAIR), bf16), vm((2, 96, PAIR), bf16), vm((2, 2, 96, PAIR), bf16),
        vm((4, 64, PAIR), f32), vm((4, 64, PAIR), f32), vm((4, 64, PAIR), f32),
        vm((6, 32, PAIR), bf16), vm((2, 32, PAIR), bf16), vm((2, 2, 32, PAIR), bf16),
        vm((NY, NC, 64, PAIR), bf16), vm((NY, NC, 128, PAIR), bf16), vm((8, 64, PAIR), f32),
        vm((HID, 1024), bf16), vm((HID, 1024), bf16), vm((HID, 1024), bf16),
        vm(part, f32), vm((2, 4, NX, ROWS, W), bf16), vm((2, 4, NX, ROWS, W), bf16),
        vm((NX, ROWS, W), bf16), vm((NX, ROWS, W), bf16),
        vm(part, f32), vm((8, 3, ROWS, W), bf16), vm((8, ROWS, W), bf16), vm((8, 2, ROWS, W), bf16),
        vm((NZ, ROWS, W), f32), vm((NZ, ROWS, W), bf16), vm((NZ, ROWS, W), bf16),
        vm((2, ROWS, W), bf16), vm((3, HID, W), bf16), vm((MOST_SENT, 8, 128), f32),
        pltpu.SemaphoreType.DMA((N_PHASES,)), pltpu.SemaphoreType.DMA((N_SEMS,)), pltpu.SemaphoreType.DMA((8,)),
    ]
    vmem = pl.BlockSpec(memory_space=pltpu.VMEM)
    anywhere = pl.BlockSpec(memory_space=pl.ANY)
    shapes = [jax.ShapeDtypeStruct((HID, W), bf16)] * 3 + [jax.ShapeDtypeStruct((ROWS, W), bf16)] * 2
    results = pl.pallas_call(
        kernel,
        out_shape=shapes,
        in_specs=[vmem] * 2 + [anywhere] * 3,
        out_specs=[anywhere] * 5,
        scratch_shapes=scratch,
        compiler_params=pltpu.CompilerParams(
            collective_id=0, has_side_effects=True, vmem_limit_bytes=60 * 1024 * 1024
        ),
    )(tokens, cotangent, gate_weight.T, up_weight.T, down_weight)
    gg, ug, dg, out, ig = pl.pallas_call(
        hand_over,
        out_shape=shapes,
        in_specs=[anywhere] * 5,
        out_specs=[anywhere] * 5,
        scratch_shapes=[vm(s.shape, s.dtype) for s in shapes] + [pltpu.SemaphoreType.DMA((10,))],
    )(*results)
    return out, ig, gg.T, ug.T, dg


def solution(mesh):
    fine = Mesh(mesh.devices.reshape(NY, NC, NZ, NX), GX + GY)
    specs = (P(GY, GX), P(GY, GX), P(GX, GY), P(GX, GY), P(GY, GX))
    return jax.shard_map(
        shards, mesh=fine, in_specs=specs, out_specs=specs, check_vma=False
    )
```

time: 113 us -> 89.8 us (0.79)
  the two profiles are of different devices: /device:TPU:64 before, /device:TPU:16 now
where the time goes in v2:
time: 89.8 us; the launch traced here: 89.6 us
  Pallas kernels  88.8 us (99%)
    pallas_call x1, Pallas kernels, shards(): pl.pallas_call(kernel, out_shape=shapes, in_specs=[vmem] * 2 + [anywhere]...  86.6 us
    pallas_call x1, Pallas kernels, shards(): pl.pallas_call(hand_over, out_shape=shapes, in_specs=[anywhere] * 5, out_...  2.19 us

profile of v2, /device:TPU:16, one launch (start us, length us, event | category | flops | bytes accessed | tf_op | source)
XLA Modules:
  0.0 89.6 jit_solution(3091284999582557196)
XLA Ops:
  0.6 86.6 %shard_map.92 = (bf16[448,512]{1,0:T(8,128)(2,1)}, bf16[448,512]{1,0:T(8,128)(2,1)}, bf16[448,512]{1,0:T(8,128)(2,1)}, bf16[32,512]{1,0:T(8,128)(2,1)}, bf16[32,512]{1,0:T(8,128)(2,1)}) custom-call(bf16[32,512]{1,0:T(8,128)(2,1)} %tok.1, bf16[32,512]{1,0:T(8,128)(2,1)} %cot.1, bf16[448,512]{1,0:T(8,128)(2,1)} %bitcast.4, bf16[448,512]{1,0:T(8,128)(2,1)} %bitcast.5, ...), custom_call_target="tpu_custom_call" | custom-call | tf_op jit(solution)/shard_map/pallas_call | solution.py:682
  87.2 2.2 %shard_map.93 = (bf16[448,512]{1,0:T(8,128)(2,1)}, bf16[448,512]{1,0:T(8,128)(2,1)}, bf16[448,512]{1,0:T(8,128)(2,1)}, bf16[32,512]{1,0:T(8,128)(2,1)}, bf16[32,512]{1,0:T(8,128)(2,1)}) custom-call(bf16[448,512]{1,0:T(8,128)(2,1)} %get-tuple-element.15.refs_0_, bf16[448,512]{1,0:T(8,128)(2,1)} %get-tuple-element.16.refs_1_, ...), custom_call_target="tpu_custom_call" | custom-call | tf_op jit(solution)/shard_map/pallas_call | solution.py:692

commit v3 on v2

--- a/solution.py
+++ b/solution.py
@@ -170,22 +170,32 @@
     def __init__(self, net, own, buf, z, x):
         self.net, self.own, self.buf, self.z, self.x = net, own, buf, z, x
         self.came, self.crossed = {}, {}
-        self.relays = net.sem()
+        self.far, self.relays = net.sem(), net.sem()
 
     def at(self, d):
         return (self.z + d + NZ) % NZ
 
     def start(self):
-        for d in (1, -1, 2, -2, 3, -3, 4):
-            h = self.net.send(self.own, self.buf.at[self.z, self.x], z=self.at(d))
-            self.came[4 if d == 4 else -d] = h
+        for d in (1, -1, 2, -2):
+            self.came[-d] = self.net.send(self.own, self.buf.at[self.z, self.x], z=self.at(d))
+
+    def forward(self, d):
+        self.came[d].wait_recv()
+        to = self.at(2 if d < 0 else -2)
+        block = self.buf.at[self.at(d), self.x]
+        if abs(d) == 1:
+            self.came[3 * d] = self.net.send(block, block, z=to)
+        else:
+            half = self.buf.at[self.at(d), self.x, pl.ds(0 if d < 0 else 16, 16)]
+            self.net.send(half, half, self.far, z=to)
 
     def cross(self, d):
         b = self.at(d)
-        src = self.own
-        if d:
+        src = self.buf.at[b, self.x] if d else self.own
+        if abs(d) == 3:
             self.came[d].wait_recv()
-            src = self.buf.at[b, self.x]
+        if d == 4:
+            self.net.wait(self.far, self.buf.at[0, 0])
         self.crossed[d] = self.net.sem()
         for k in (1, 3):
             self.net.send(src, self.buf.at[b, self.x], self.crossed[d], x=(self.x + k) % NX)
@@ -219,9 +229,12 @@
         send, y = self.net.send, self.y
         self.p0 = send(self.part(y, 0), self.part(y, 0), y=self.yp)
         self.m1 = send(self.part(y, 1), self.part(y, 1), y=self.ym)
+        self.own = self.to_pair(y)
+
+    def start_rest(self):
+        send, y = self.net.send, self.y
         self.p1 = send(self.part(y, 1), self.part(y, 1), y=self.yp)
         self.m0 = send(self.part(y, 0), self.part(y, 0), y=self.ym)
-        self.own = self.to_pair(y)
 
     def relay(self):
         send = self.net.send
@@ -244,10 +257,10 @@
         self.net.wait(self.pair, self.buf.at[:, 0])
 
 
-N_SEMS = 110
+N_SEMS = 118
 N_PHASES = 5
 MOST_SENT = 1280
-RELATIVE = (4, 3, -3, 2, -2, 1, -1, 0)
+RELATIVE = (3, -3, 2, -2, 1, -1, 4, 0)
 
 
 def kernel(
@@ -257,7 +270,7 @@
     pk_src, pk_buf, ph_src, ph_buf, pk, ph,
     dsrc, drecv, acc, ysrc, yrel, yfin, esrc, erecv, eacc, bsrc, brel, bfin,
     h_all, a_all, hrot, cht, gat, uat,
-    o_part, osrc, orecv, oxs, oxr,
+    o_part, osrc, orecv, oxs, oxr, lsrc, lrel, lfin, lzs, lzr,
     i_part, isrc, irel, ifin, izf, izs, izr,
     small, grads, unread,
     ssem, rsem, lsem,
@@ -319,34 +332,37 @@
     T.start()
     peaks.start(own_peaks)
     T.cross(0)
+    T.forward(1)
+    T.forward(-1)
+    peaks.second()
     T.cross(1)
     T.cross(-1)
+    for d in (2, -2):
+        T.forward(d)
+        T.cross(d)
     T.relay(0)
-    peaks.second()
-    T.cross(2)
-    T.cross(-2)
+    net.phase = 1
+    C.start()
     T.relay(1)
     T.relay(-1)
-    peaks.third()
-    net.phase = 1
-    C.start()
     T.cross(3)
     T.cross(-3)
+    T.cross(4)
     T.relay(2)
     T.relay(-2)
-    T.cross(4)
+    peaks.third()
+    for d in (1, -1, 2, -2):
+        C.forward(d)
     T.relay(3)
     T.relay(-3)
-    C.cross(0)
+    T.relay(4)
+    for d in (0, 1, -1, 2, -2):
+        C.cross(d)
     pk[...] = peaks.result()
     inv_x = 1.0 / (pk[0:1, 0:1] + TINY)
     cg[...] = (TOP * jnp.tanh(rg[...] * (1.0 / (pk[1:2, 0:1] + TINY)))).astype(bf16)
     cu[...] = (TOP * jnp.tanh(ru[...] * (1.0 / (pk[2:3, 0:1] + TINY)))).astype(bf16)
-    T.relay(4)
     T.done()
-    C.cross(1)
-    C.cross(-1)
-    C.relay(0)
 
     def gate_up(k, dst):
         t = turn_cols(t_all[k].reshape(4 * ROWS, W), h128)
@@ -358,9 +374,11 @@
     order = [y2, yp, ym, y]
     dh, eh = {}, {}
 
-    def both(i):
+    def pair_part(i):
         gate_up(order[i] * 2 + pc, dsrc.at[i])
         dh[i] = send(dsrc.at[i], drecv.at[i], c=pc)
+
+    def own_part(i):
         gate_up(order[i] * 2 + c, acc.at[i])
 
     def q(i, at):
@@ -372,34 +390,37 @@
 
     net.phase = 2
     y_fin, b_fin = net.sem(), net.sem()
-    both(0)
-    both(1)
+    pair_part(0)
+    pair_part(1)
+    own_part(0)
+    C.cross(3)
+    C.cross(-3)
+    C.cross(4)
     dh[0].wait_recv()
     relp = put(0, q(0, 0), yrel.at[0], y=yp)
     relm = put(1, q(0, 64), yrel.at[1], y=ym)
-    both(2)
+    own_part(1)
+    pair_part(2)
+    C.relay(0)
+    C.relay(1)
+    C.relay(-1)
+    own_part(2)
     dh[1].wait_recv()
     put(2, q(1, 64), yfin.at[0, 1], y_fin, y=yp)
     dh[2].wait_recv()
     put(3, q(2, 0), yfin.at[1, 0], y_fin, y=ym)
-    C.cross(2)
-    C.cross(-2)
-    C.relay(1)
-    C.relay(-1)
-    cd[...] = (TOP * jnp.tanh(rd[...] * (1.0 / (pk[3:4, 0:1] + TINY)))).astype(bf16)
-    C.cross(3)
-    C.cross(-3)
     C.relay(2)
     C.relay(-2)
-    C.cross(4)
+    cd[...] = (TOP * jnp.tanh(rd[...] * (1.0 / (pk[3:4, 0:1] + TINY)))).astype(bf16)
+    pair_part(3)
+    C.relay(3)
+    C.relay(-3)
+    C.relay(4)
     relp.wait_recv()
     put(4, q(1, 0) + decode(yrel.at[0]), yfin.at[0, 0], y_fin, y=yp)
     relm.wait_recv()
     put(5, q(2, 64) + decode(yrel.at[1]), yfin.at[1, 1], y_fin, y=ym)
-    both(3)
-    C.relay(3)
-    C.relay(-3)
-    C.relay(4)
+    own_part(3)
     C.done()
 
     def back(k, dst):
@@ -407,11 +428,6 @@
         dst[:, 0:HID] = b[0:64]
         dst[:, HID:PAIR] = b[64:128]
 
-    def both_back(i):
-        back(order[i] * 2 + pc, esrc.at[i])
-        eh[i] = send(esrc.at[i], erecv.at[i], c=pc)
-        back(order[i] * 2 + c, eacc.at[i])
-
     def e(i, at):
         return eacc[i, at : at + 32] + erecv[i, at : at + 32]
 
@@ -419,89 +435,21 @@
         bsrc[slot] = v.astype(bf16)
         return send(bsrc.at[slot], dst, sem, **dev)
 
-    both_back(0)
-    both_back(1)
-    eh[0].wait_recv()
-    brp = put_b(0, e(0, 0), brel.at[0], y=yp)
-    brm = put_b(1, e(0, 32), brel.at[1], y=ym)
-    both_back(2)
+    for i in range(4):
+        back(order[i] * 2 + pc, esrc.at[i])
+        eh[i] = send(esrc.at[i], erecv.at[i], c=pc)
+    for i in range(4):
+        back(order[i] * 2 + c, eacc.at[i])
+        if i == 0:
+            eh[0].wait_recv()
+            brp = put_b(0, e(0, 0), brel.at[0], y=yp)
+            brm = put_b(1, e(0, 32), brel.at[1], y=ym)
     eh[1].wait_recv()
     put_b(2, e(1, 32), bfin.at[0, 1], b_fin, y=yp)
     eh[2].wait_recv()
     put_b(3, e(2, 0), bfin.at[1, 0], b_fin, y=ym)
-    both_back(3)
-
-    dh[3].wait_recv()
-    net.wait(y_fin, yfin)
-    for i in range(2):
-        acc[3, 64 * i : 64 * i + 64] = q(3, 64 * i) + decode(yfin.at[0, i]) + decode(yfin.at[1, i])
+
     p_x, p_g, p_u, p_d = (pk[i : i + 1, 0:1] for i in range(4))
-    gate = acc[3, :, 0:HID] * (p_x * p_g / (TOP * TOP))
-    up = acc[3, :, HID:PAIR] * (p_x * p_u / (TOP * TOP))
-    s = jax.nn.sigmoid(gate)
-    hid = (gate * s * up).astype(bf16)
-    h_all[y, c, :, 0:HID] = hid[0:64]
-    h_all[y, c, :, HID:PAIR] = hid[64:128]
-    hidp = Peaks(net, ph_src, ph_buf, (y, c, z, x))
-    p_h = jnp.max(jnp.abs(turn_cols(hid, h64))) * R64
-    hidp.start(jnp.full((8, 128), p_h, f32))
-    net.phase = 3
-    H = Gather(net, h_all, 32, y, c, True)
-    H.start()
-    brp.wait_recv()
-    put_b(4, e(1, 0) + brel[0].astype(f32), bfin.at[0, 0], b_fin, y=yp)
-    brm.wait_recv()
-    put_b(5, e(2, 32) + brel[1].astype(f32), bfin.at[1, 1], b_fin, y=ym)
-    hidp.second()
-    H.relay()
-    eh[3].wait_recv()
-    net.wait(b_fin, bfin)
-    b = jnp.concatenate(
-        [e(3, 32 * i) + bfin[0, i].astype(f32) + bfin[1, i].astype(f32) for i in range(2)], axis=0
-    )
-    b = turn_cols(b * (p_d / TOP), h64, 3) * R64
-    hg = jnp.concatenate([b[:, 0:HID], b[:, HID:PAIR]], axis=0)
-    a_all[y, c, :, 0:HID] = (hg * up * s * (1.0 + gate * (1.0 - s))).astype(bf16)
-    a_all[y, c, :, HID:PAIR] = (hg * gate * s).astype(bf16)
-    G = Gather(net, a_all, 64, y, c, False)
-    G.start()
-    hidp.third()
-    H.share()
-    H.last()
-    H.done()
-
-    def turn_hidden(k, carry):
-        hrot[k] = turn_cols(h_all[k // 2, k % 2], h64) * R64
-        return carry
-
-    lax.fori_loop(0, 8, turn_hidden, 0)
-    ph[...] = hidp.result()
-    p_h = ph[0:1, 0:1]
-    inv_h = 1.0 / (p_h + TINY)
-
-    def o_block(d):
-        k = zat(d)
-        v = (TOP * jnp.tanh(hrot[k] * inv_h)).astype(bf16)
-        v = jnp.concatenate([v[:, 0:HID], v[:, HID:PAIR]], axis=0)
-        cht[:, pl.ds(pl.multiple_of(k * 128, 128), 128)] = v.T
-        o_part[RELATIVE.index(d)] = mm(v, cd[...]).reshape(NX, ROWS, W)
-
-    op, om = {}, {}
-    o_last, o_cross = net.sem(), net.sem()
-
-    def o_ring(s):
-        for side, d, handles, dev in ((0, 4 - s, op, zp), (1, s - 4, om, zm)):
-            i = RELATIVE.index(4 if s == 0 else d)
-            for j in (2, 3, 0, 1) if side == 0 else (0, 1, 2, 3):
-                if s == 0 and (j < 2) != (side == 0):
-                    continue
-                v = o_part[i, j]
-                if (s - 1, j) in handles:
-                    handles[s - 1, j].wait_recv()
-                    v = v + orecv[side, s - 1, j].astype(f32)
-                osrc[side, s, j] = v.astype(bf16)
-                sem = o_last if s == 3 else None
-                handles[s, j] = send(osrc.at[side, s, j], orecv.at[side, s, j], sem, z=dev)
 
     blocks = [(y, c), (y, pc), (ym, c), (yp, c), (ym, pc), (yp, pc), (y2, c), (y2, pc)]
     ir = {}
@@ -549,48 +497,170 @@
         def _():
             net.copy(izs.at[d], izr.at[d], i_owner, z=k).start()
 
+    dh[3].wait_recv()
+    net.wait(y_fin, yfin)
+    for i in range(2):
+        acc[3, 64 * i : 64 * i + 64] = q(3, 64 * i) + decode(yfin.at[0, i]) + decode(yfin.at[1, i])
+    gate = acc[3, :, 0:HID] * (p_x * p_g / (TOP * TOP))
+    up = acc[3, :, HID:PAIR] * (p_x * p_u / (TOP * TOP))
+    s = jax.nn.sigmoid(gate)
+    hid = (gate * s * up).astype(bf16)
+    h_all[y, c, :, 0:HID] = hid[0:64]
+    h_all[y, c, :, HID:PAIR] = hid[64:128]
+    hidp = Peaks(net, ph_src, ph_buf, (y, c, z, x))
+
+    def turn_hidden(yy, cc):
+        hrot[yy * 2 + cc] = turn_cols(h_all[yy, cc], h64) * R64
+
+    turn_hidden(y, c)
+    p_h = jnp.max(jnp.abs(hrot[y * 2 + c]))
+    hidp.start(jnp.full((8, 128), p_h, f32))
+    net.phase = 3
+    H = Gather(net, h_all, 32, y, c, True)
+    H.start()
+    brp.wait_recv()
+    put_b(4, e(1, 0) + brel[0].astype(f32), bfin.at[0, 0], b_fin, y=yp)
+    brm.wait_recv()
+    put_b(5, e(2, 32) + brel[1].astype(f32), bfin.at[1, 1], b_fin, y=ym)
+    H.start_rest()
+    hidp.second()
+    H.relay()
+    eh[3].wait_recv()
+    net.wait(b_fin, bfin)
+    b = jnp.concatenate(
+        [e(3, 32 * i) + bfin[0, i].astype(f32) + bfin[1, i].astype(f32) for i in range(2)], axis=0
+    )
+    b = turn_cols(b * (p_d / TOP), h64, 3) * R64
+    hg = jnp.concatenate([b[:, 0:HID], b[:, HID:PAIR]], axis=0)
+    a_all[y, c, :, 0:HID] = (hg * up * s * (1.0 + gate * (1.0 - s))).astype(bf16)
+    a_all[y, c, :, HID:PAIR] = (hg * gate * s).astype(bf16)
+    G = Gather(net, a_all, 64, y, c, False)
+    G.start()
+    G.start_rest()
+    H.share()
+    hidp.third()
+    H.last()
+    for yy in (ym, yp, y2):
+        turn_hidden(yy, c)
+    H.done()
+    for yy in (y, ym, yp, y2):
+        turn_hidden(yy, pc)
     net.phase = 4
+    i_block(0)
+    ph[...] = hidp.result()
+    p_h = ph[0:1, 0:1]
+    inv_h = 1.0 / (p_h + TINY)
+
+    def o_block(d):
+        k = zat(d)
+        v = (TOP * jnp.tanh(hrot[k] * inv_h)).astype(bf16)
+        v = jnp.concatenate([v[:, 0:HID], v[:, HID:PAIR]], axis=0)
+        cht[:, pl.ds(pl.multiple_of(k * 128, 128), 128)] = v.T
+        o_part[RELATIVE.index(d)] = mm(v, cd[...]).reshape(NX, ROWS, W)
+
+    left_r = {}
+    left_fin = [net.sem() for _ in range(4)]
+    left_owner = net.sem()
+
+    def left_send(g, way, dst, sem=None):
+        to = xp if way == 1 else xm
+        return send(lsrc.at[g, 0 if sem is None else way], dst, sem, x=to)
+
+    def left_start(g):
+        way = 1 if g % 2 == 0 else 2
+        for i in range(2):
+            lsrc[g, 0, i] = o_part[2 * g + i, x2, :, 0:256].astype(bf16)
+        left_r[g] = left_send(g, way, lrel.at[g])
+        for i in range(2):
+            lsrc[g, 3 - way, i] = o_part[2 * g + i, xp if way == 2 else xm, :, 0:256].astype(bf16)
+        left_send(g, 3 - way, lfin.at[g, 2 - way], left_fin[g])
+
+    def left_relay(g):
+        way = 1 if g % 2 == 0 else 2
+        left_r[g].wait_recv()
+        for i in range(2):
+            v = o_part[2 * g + i, xp if way == 1 else xm, :, 0:256] + lrel[g, i].astype(f32)
+            lsrc[g, way, i] = v.astype(bf16)
+        left_send(g, way, lfin.at[g, way - 1], left_fin[g])
+
+    def left_final(g):
+        net.wait(left_fin[g], lfin.at[g])
+        for i in range(2):
+            n = 2 * g + i
+            v = o_part[n, x, :, 0:256] + lfin[g, 0, i].astype(f32) + lfin[g, 1, i].astype(f32)
+            if n == 7:
+                o_part[7, x, :, 0:256] = v
+            else:
+                lzs[n] = v.astype(bf16)
+                send(lzs.at[n], lzr.at[n], left_owner, z=zat(RELATIVE[n]))
+
+    op, om = {}, {}
+    o_last, o_cross = net.sem(), net.sem()
+
+    def o_ring(s):
+        for side, d, handles, dev in ((0, 4 - s, op, zp), (1, s - 4, om, zm)):
+            i = RELATIVE.index(4 if s == 0 else d)
+            for j in (2, 3, 0, 1) if side == 0 else (0, 1, 2, 3):
+                if s == 0 and (j < 2) != (side == 0):
+                    continue
+                v = o_part[i, j, :, 256:512]
+                if (s - 1, j) in handles:
+                    handles[s - 1, j].wait_recv()
+                    v = v + orecv[side, s - 1, j].astype(f32)
+                osrc[side, s, j] = v.astype(bf16)
+                sem = o_last if s == 3 else None
+                handles[s, j] = send(osrc.at[side, s, j], orecv.at[side, s, j], sem, z=dev)
+
     o_block(4)
     o_ring(0)
     G.relay()
-    i_block(0)
+    o_block(3)
+    o_block(-3)
+    left_start(0)
+    o_block(2)
+    o_block(-2)
+    left_start(1)
     G.own.wait_recv()
     i_block(1)
+    o_ring(1)
     G.share()
-    o_block(3)
-    o_block(-3)
-    o_ring(1)
+    o_block(1)
+    o_block(-1)
+    left_start(2)
+    o_block(0)
+    left_start(3)
+    left_relay(0)
+    left_relay(1)
+    i_relay(0)
+    i_relay(1)
     i_block(2)
     i_block(3)
-    i_relay(0)
-    i_relay(1)
-    o_block(2)
-    o_block(-2)
     G.last()
-    o_ring(2)
-    i_final(0)
-    i_final(1)
     G.fp.wait_recv()
     i_block(4)
     G.fm.wait_recv()
     i_block(5)
-    i_relay(2)
-    i_relay(3)
-    o_block(1)
-    o_block(-1)
+    o_ring(2)
     i_block(6)
     G.f2.wait_recv()
     i_block(7)
+    left_relay(2)
+    left_relay(3)
+    left_final(0)
+    left_final(1)
+    i_relay(2)
+    i_relay(3)
     o_ring(3)
+    i_final(0)
+    i_final(1)
+    i_relay(4)
+    i_relay(5)
+    left_final(2)
+    left_final(3)
+    i_relay(6)
+    i_relay(7)
     i_final(2)
     i_final(3)
-    i_relay(4)
-    i_relay(5)
-    o_block(0)
-    i_relay(6)
-    i_relay(7)
-    i_final(4)
-    i_final(5)
 
     stores = []
 
@@ -599,28 +669,40 @@
         copy.start()
         stores.append(copy)
 
+    def weight_grad(i, acts, dst):
+        for at, n in cut(HID):
+            v = mm(acts[at : at + n], tc[...].reshape(1024, W)) * (p_x / TOP)
+            grads[i, at : at + n] = (turn_cols(v, h128, 2) * R128).astype(bf16)
+        store(grads.at[i], dst)
+
+    net.wait(o_last, orecv.at[:, 3])
+    for j in range(NX):
+        v = o_part[7, j, :, 256:512] + orecv[0, 3, j].astype(f32) + orecv[1, 3, j].astype(f32)
+        o_part[7, j, :, 256:512] = v
+        oxs[j] = v.astype(bf16)
+    for j in range(1, NX):
+        send(oxs.at[(x + j) % NX], oxr.at[j], o_cross, x=(x + j) % NX)
     for at, n in cut(HID):
         v = mm(cht[at : at + n], c_all[...].reshape(1024, W)) * (p_h / TOP)
         grads[2, at : at + n] = (sum(mm(h64[:n, :n], p) for p in split(v, 2)) * R64).astype(bf16)
     store(grads.at[2], dg_hbm)
-    net.wait(o_last, orecv.at[:, 3])
-    for j in range(NX):
-        o_part[7, j] = o_part[7, j] + orecv[0, 3, j].astype(f32) + orecv[1, 3, j].astype(f32)
-        oxs[j] = o_part[7, j].astype(bf16)
-    for j in range(1, NX):
-        send(oxs.at[(x + j) % NX], oxr.at[j], o_cross, x=(x + j) % NX)
+    i_final(4)
+    i_final(5)
+    weight_grad(0, gat, gg_hbm)
     i_final(6)
     i_final(7)
-    for i, (acts, dst) in enumerate(((gat, gg_hbm), (uat, ug_hbm))):
-        for at, n in cut(HID):
-            v = mm(acts[at : at + n], tc[...].reshape(1024, W)) * (p_x / TOP)
-            grads[i, at : at + n] = (turn_cols(v, h128, 2) * R128).astype(bf16)
-        store(grads.at[i], dst)
-    v = o_part[7, x]
+    weight_grad(1, uat, ug_hbm)
+    scale = p_h * p_d / (TOP * TOP)
     net.wait(o_cross, oxr.at[pl.ds(1, NX - 1)])
+    v = o_part[7, x, :, 256:512]
     for j in range(1, NX):
         v = v + oxr[j].astype(f32)
-    small[0] = (v * (p_h * p_d / (TOP * TOP))).astype(bf16)
+    small[0, :, 256:512] = (v * scale).astype(bf16)
+    net.wait(left_owner, lzr)
+    v = o_part[7, x, :, 0:256]
+    for n in range(7):
+        v = v + lzr[n].astype(f32)
+    small[0, :, 0:256] = (v * scale).astype(bf16)
     store(small.at[0], out_hbm)
     v = izf[0]
     net.count(izs.at[0], NZ - 1)
@@ -669,8 +751,10 @@
         vm((6, 32, PAIR), bf16), vm((2, 32, PAIR), bf16), vm((2, 2, 32, PAIR), bf16),
         vm((NY, NC, 64, PAIR), bf16), vm((NY, NC, 128, PAIR), bf16), vm((8, 64, PAIR), f32),
         vm((HID, 1024), bf16), vm((HID, 1024), bf16), vm((HID, 1024), bf16),
-        vm(part, f32), vm((2, 4, NX, ROWS, W), bf16), vm((2, 4, NX, ROWS, W), bf16),
-        vm((NX, ROWS, W), bf16), vm((NX, ROWS, W), bf16),
+        vm(part, f32), vm((2, 4, NX, ROWS, 256), bf16), vm((2, 4, NX, ROWS, 256), bf16),
+        vm((NX, ROWS, 256), bf16), vm((NX, ROWS, 256), bf16),
+        vm((4, 3, 2, ROWS, 256), bf16), vm((4, 2, ROWS, 256), bf16), vm((4, 2, 2, ROWS, 256), bf16),
+        vm((7, ROWS, 256), bf16), vm((7, ROWS, 256), bf16),
         vm(part, f32), vm((8, 3, ROWS, W), bf16), vm((8, ROWS, W), bf16), vm((8, 2, ROWS, W), bf16),
         vm((NZ, ROWS, W), f32), vm((NZ, ROWS, W), bf16), vm((NZ, ROWS, W), bf16),
         vm((2, ROWS, W), bf16), vm((3, HID, W), bf16), vm((MOST_SENT, 8, 128), f32),

time: 89.8 us -> 82.3 us (0.916)
  Pallas kernels: 88.8 us -> 81.2 us
    pallas_call x1, Pallas kernels: 86.6 us -> 79.1 us  [shards(): pl.pallas_call(kernel, out_shape=shapes, in_specs=[vmem] * 2 + [anywhere]...]
where the time goes in v3:
time: 82.3 us; the launch traced here: 82 us
  Pallas kernels  81.2 us (99%)
    pallas_call x1, Pallas kernels, shards(): pl.pallas_call(kernel, out_shape=shapes, in_specs=[vmem] * 2 + [anywhere]...  79.1 us
    pallas_call x1, Pallas kernels, shards(): pl.pallas_call(hand_over, out_shape=shapes, in_specs=[anywhere] * 5, out_...  2.19 us

profile of v3, /device:TPU:16, one launch (start us, length us, event | category | flops | bytes accessed | tf_op | source)
XLA Modules:
  0.0 82.0 jit_solution(6495375057312283431)
XLA Ops:
  0.6 79.1 %shard_map.92 = (bf16[448,512]{1,0:T(8,128)(2,1)}, bf16[448,512]{1,0:T(8,128)(2,1)}, bf16[448,512]{1,0:T(8,128)(2,1)}, bf16[32,512]{1,0:T(8,128)(2,1)}, bf16[32,512]{1,0:T(8,128)(2,1)}) custom-call(bf16[32,512]{1,0:T(8,128)(2,1)} %tok.1, bf16[32,512]{1,0:T(8,128)(2,1)} %cot.1, bf16[448,512]{1,0:T(8,128)(2,1)} %bitcast.4, bf16[448,512]{1,0:T(8,128)(2,1)} %bitcast.5, ...), custom_call_target="tpu_custom_call" | custom-call | tf_op jit(solution)/shard_map/pallas_call | solution.py:766
  79.7 2.2 %shard_map.93 = (bf16[448,512]{1,0:T(8,128)(2,1)}, bf16[448,512]{1,0:T(8,128)(2,1)}, bf16[448,512]{1,0:T(8,128)(2,1)}, bf16[32,512]{1,0:T(8,128)(2,1)}, bf16[32,512]{1,0:T(8,128)(2,1)}) custom-call(bf16[448,512]{1,0:T(8,128)(2,1)} %get-tuple-element.15.refs_0_, bf16[448,512]{1,0:T(8,128)(2,1)} %get-tuple-element.16.refs_1_, ...), custom_call_target="tpu_custom_call" | custom-call | tf_op jit(solution)/shard_map/pallas_call | solution.py:776

commit v4 on v3

--- a/solution.py
+++ b/solution.py
@@ -260,19 +260,19 @@
 N_SEMS = 118
 N_PHASES = 5
 MOST_SENT = 1280
-RELATIVE = (3, -3, 2, -2, 1, -1, 4, 0)
+RELATIVE = (3, -3, 4, 0, 2, -2, 1, -1)
 
 
 def kernel(
-    tok, cot, wg_hbm, wu_hbm, wd_hbm,
-    gg_hbm, ug_hbm, dg_hbm, out_hbm, ig_hbm,
-    h128, h64, wts, t_all, c_all, tc, rg, ru, rd, cg, cu, cd,
+    tok_hbm, cot_hbm, wg_hbm, wu_hbm, wd_hbm,
+    gg, ug, dg, out, ig,
+    tok, cot, h128, h64, wts, t_all, c_all, tc, rg, ru, rd, cg, cu, cd,
     pk_src, pk_buf, ph_src, ph_buf, pk, ph,
     dsrc, drecv, acc, ysrc, yrel, yfin, esrc, erecv, eacc, bsrc, brel, bfin,
     h_all, a_all, hrot, cht, gat, uat,
     o_part, osrc, orecv, oxs, oxr, lsrc, lrel, lfin, lzs, lzr,
     i_part, isrc, irel, ifin, izf, izs, izr,
-    small, grads, unread,
+    unread,
     ssem, rsem, lsem,
 ):
     y = lax.axis_index("gx_0")
@@ -300,16 +300,22 @@
     for j in range(1, NZ):
         pl.semaphore_signal(barrier, inc=1, device_id={"gy_0": (z + j) % NZ}, device_id_type=MESH)
     loads = [
-        pltpu.make_async_copy(w, wts.at[i], lsem.at[i]) for i, w in enumerate((wg_hbm, wu_hbm, wd_hbm))
+        pltpu.make_async_copy(src, dst, lsem.at[i])
+        for i, (src, dst) in enumerate(
+            (
+                (tok_hbm, tok), (cot_hbm, cot),
+                (wg_hbm, wts.at[0]), (wu_hbm, wts.at[1]), (wd_hbm, wts.at[2]),
+            )
+        )
     ]
     for load in loads:
         load.start()
     h128[...] = table(256, 128)
     h64[...] = table(256, 64)
+    for load in loads:
+        load.wait()
     t_all[z, x] = tok[...]
     c_all[z, x] = cot[...]
-    for load in loads:
-        load.wait()
 
     def rotate_weights():
         rg[...] = turn_cols(wts[0], h128) * R128
@@ -376,7 +382,12 @@
 
     def pair_part(i):
         gate_up(order[i] * 2 + pc, dsrc.at[i])
-        dh[i] = send(dsrc.at[i], drecv.at[i], c=pc)
+        if i == 0:
+            first, last = pl.ds(0, 64), pl.ds(64, 64)
+            dh["first"] = send(dsrc.at[0, first], drecv.at[0, first], c=pc)
+            dh[0] = send(dsrc.at[0, last], drecv.at[0, last], c=pc)
+        else:
+            dh[i] = send(dsrc.at[i], drecv.at[i], c=pc)
 
     def own_part(i):
         gate_up(order[i] * 2 + c, acc.at[i])
@@ -396,8 +407,9 @@
     C.cross(3)
     C.cross(-3)
     C.cross(4)
+    dh["first"].wait_recv()
+    relp = put(0, q(0, 0), yrel.at[0], y=yp)
     dh[0].wait_recv()
-    relp = put(0, q(0, 0), yrel.at[0], y=yp)
     relm = put(1, q(0, 64), yrel.at[1], y=ym)
     own_part(1)
     pair_part(2)
@@ -537,16 +549,21 @@
     G = Gather(net, a_all, 64, y, c, False)
     G.start()
     G.start_rest()
+    net.phase = 4
+    i_block(0)
     H.share()
     hidp.third()
+    G.own.wait_recv()
+    i_block(1)
     H.last()
     for yy in (ym, yp, y2):
         turn_hidden(yy, c)
     H.done()
     for yy in (y, ym, yp, y2):
         turn_hidden(yy, pc)
-    net.phase = 4
-    i_block(0)
+    G.relay()
+    i_relay(0)
+    i_relay(1)
     ph[...] = hidp.result()
     p_h = ph[0:1, 0:1]
     inv_h = 1.0 / (p_h + TINY)
@@ -560,7 +577,8 @@
 
     left_r = {}
     left_fin = [net.sem() for _ in range(4)]
-    left_owner = net.sem()
+    left_owner, left_mid = net.sem(), net.sem()
+    ZERO = RELATIVE.index(0)
 
     def left_send(g, way, dst, sem=None):
         to = xp if way == 1 else xm
@@ -585,14 +603,28 @@
 
     def left_final(g):
         net.wait(left_fin[g], lfin.at[g])
+        if g == 2:
+            net.wait(left_mid, lzr.at[pl.ds(0, 3)])
         for i in range(2):
-            n = 2 * g + i
+            n, d = 2 * g + i, RELATIVE[2 * g + i]
             v = o_part[n, x, :, 0:256] + lfin[g, 0, i].astype(f32) + lfin[g, 1, i].astype(f32)
-            if n == 7:
-                o_part[7, x, :, 0:256] = v
+            if abs(d) == 2:
+                v = v + lzr[0 if d > 0 else 1].astype(f32)
+                half = lzr[2].astype(f32)
+                rows = lax.broadcasted_iota(jnp.int32, (ROWS, 256), 0)
+                v = v + jnp.where((rows < 16) if d > 0 else (rows >= 16), half, 0.0)
+            if d == 0:
+                o_part[n, x, :, 0:256] = v
+                continue
+            lzs[n] = v.astype(bf16)
+            if d == 4:
+                for at, to in ((0, 2), (16, -2)):
+                    rows = pl.ds(at, 16)
+                    send(lzs.at[n, rows], lzr.at[2, rows], left_mid, z=zat(to))
+            elif abs(d) == 3:
+                send(lzs.at[n], lzr.at[0 if d > 0 else 1], left_mid, z=zat(d // 3))
             else:
-                lzs[n] = v.astype(bf16)
-                send(lzs.at[n], lzr.at[n], left_owner, z=zat(RELATIVE[n]))
+                send(lzs.at[n], lzr.at[3 + RELATIVE[4:].index(d)], left_owner, z=zat(d))
 
     op, om = {}, {}
     o_last, o_cross = net.sem(), net.sem()
@@ -613,26 +645,23 @@
 
     o_block(4)
     o_ring(0)
-    G.relay()
     o_block(3)
     o_block(-3)
     left_start(0)
+    o_block(0)
+    left_start(1)
+    i_final(0)
+    i_final(1)
     o_block(2)
     o_block(-2)
-    left_start(1)
-    G.own.wait_recv()
-    i_block(1)
     o_ring(1)
     G.share()
+    left_start(2)
     o_block(1)
     o_block(-1)
-    left_start(2)
-    o_block(0)
     left_start(3)
     left_relay(0)
     left_relay(1)
-    i_relay(0)
-    i_relay(1)
     i_block(2)
     i_block(3)
     G.last()
@@ -644,93 +673,70 @@
     i_block(6)
     G.f2.wait_recv()
     i_block(7)
-    left_relay(2)
-    left_relay(3)
     left_final(0)
     left_final(1)
     i_relay(2)
     i_relay(3)
+    left_relay(2)
+    left_relay(3)
     o_ring(3)
-    i_final(0)
-    i_final(1)
     i_relay(4)
     i_relay(5)
-    left_final(2)
-    left_final(3)
     i_relay(6)
     i_relay(7)
     i_final(2)
     i_final(3)
-
-    stores = []
-
-    def store(src, dst):
-        copy = pltpu.make_async_copy(src, dst, lsem.at[3 + len(stores)])
-        copy.start()
-        stores.append(copy)
-
-    def weight_grad(i, acts, dst):
+    left_final(2)
+    left_final(3)
+
+    def weight_grad(acts, dst):
         for at, n in cut(HID):
             v = mm(acts[at : at + n], tc[...].reshape(1024, W)) * (p_x / TOP)
-            grads[i, at : at + n] = (turn_cols(v, h128, 2) * R128).astype(bf16)
-        store(grads.at[i], dst)
+            dst[at : at + n] = (turn_cols(v, h128, 2) * R128).astype(bf16)
 
     net.wait(o_last, orecv.at[:, 3])
     for j in range(NX):
-        v = o_part[7, j, :, 256:512] + orecv[0, 3, j].astype(f32) + orecv[1, 3, j].astype(f32)
-        o_part[7, j, :, 256:512] = v
+        v = o_part[ZERO, j, :, 256:512] + orecv[0, 3, j].astype(f32) + orecv[1, 3, j].astype(f32)
+        o_part[ZERO, j, :, 256:512] = v
         oxs[j] = v.astype(bf16)
     for j in range(1, NX):
         send(oxs.at[(x + j) % NX], oxr.at[j], o_cross, x=(x + j) % NX)
+    i_final(4)
+    i_final(5)
+    i_final(6)
+    i_final(7)
     for at, n in cut(HID):
         v = mm(cht[at : at + n], c_all[...].reshape(1024, W)) * (p_h / TOP)
-        grads[2, at : at + n] = (sum(mm(h64[:n, :n], p) for p in split(v, 2)) * R64).astype(bf16)
-    store(grads.at[2], dg_hbm)
-    i_final(4)
-    i_final(5)
-    weight_grad(0, gat, gg_hbm)
-    i_final(6)
-    i_final(7)
-    weight_grad(1, uat, ug_hbm)
+        dg[at : at + n] = (sum(mm(h64[:n, :n], p) for p in split(v, 2)) * R64).astype(bf16)
+    weight_grad(gat, gg)
+    weight_grad(uat, ug)
     scale = p_h * p_d / (TOP * TOP)
     net.wait(o_cross, oxr.at[pl.ds(1, NX - 1)])
-    v = o_part[7, x, :, 256:512]
+    v = o_part[ZERO, x, :, 256:512]
     for j in range(1, NX):
         v = v + oxr[j].astype(f32)
-    small[0, :, 256:512] = (v * scale).astype(bf16)
-    net.wait(left_owner, lzr)
-    v = o_part[7, x, :, 0:256]
-    for n in range(7):
+    out[:, 256:512] = (v * scale).astype(bf16)
+    net.wait(left_owner, lzr.at[pl.ds(3, 4)])
+    v = o_part[ZERO, x, :, 0:256]
+    for n in range(3, 7):
         v = v + lzr[n].astype(f32)
-    small[0, :, 0:256] = (v * scale).astype(bf16)
-    store(small.at[0], out_hbm)
+    out[:, 0:256] = (v * scale).astype(bf16)
     v = izf[0]
     net.count(izs.at[0], NZ - 1)
     net.wait(i_owner, izr.at[pl.ds(1, NZ - 1)])
     for d in range(1, NZ):
         v = v + izr[d].astype(f32)
-    small[1] = (turn_cols(v, h128, 3) * R128).astype(bf16)
-    store(small.at[1], ig_hbm)
+    ig[...] = (turn_cols(v, h128, 3) * R128).astype(bf16)
     net.wait_sent(unread)
-    for copy in stores:
+
+
+def hand_over(*refs):
+    n = len(refs) // 2
+    copies = [pltpu.make_async_copy(refs[i], refs[n + i], refs[-1].at[i]) for i in range(n)]
+    for copy in copies:
+        copy.start()
+    for copy in copies:
         copy.wait()
-
-
-def hand_over(*refs):
-    n = len(refs) // 3
-    given, sems = refs[: 2 * n], refs[-1]
-    kept = refs[2 * n : 3 * n]
-    copies = []
-    for i in range(n):
-        copies.append(pltpu.make_async_copy(given[i], kept[i], sems.at[i]))
-        copies[i].start()
-    outs = []
-    for i in range(n):
-        copies[i].wait()
-        outs.append(pltpu.make_async_copy(kept[i], given[n + i], sems.at[n + i]))
-        outs[i].start()
-    for out in outs:
-        out.wait()
 
 
 def shards(tokens, cotangent, gate_weight, up_weight, down_weight):
@@ -739,6 +745,7 @@
 
     part = (NZ, NX, ROWS, W)
     scratch = [
+        vm((ROWS, W), bf16), vm((ROWS, W), bf16),
         vm((256, 256), bf16), vm((256, 256), bf16), vm((3, HID, W), bf16),
         vm(part, bf16), vm(part, bf16), vm((8, 128, W), bf16),
         vm((HID, W), f32), vm((HID, W), f32), vm((HID, W), f32),
@@ -754,31 +761,33 @@
         vm(part, f32), vm((2, 4, NX, ROWS, 256), bf16), vm((2, 4, NX, ROWS, 256), bf16),
         vm((NX, ROWS, 256), bf16), vm((NX, ROWS, 256), bf16),
         vm((4, 3, 2, ROWS, 256), bf16), vm((4, 2, ROWS, 256), bf16), vm((4, 2, 2, ROWS, 256), bf16),
-        vm((7, ROWS, 256), bf16), vm((7, ROWS, 256), bf16),
+        vm((8, ROWS, 256), bf16), vm((7, ROWS, 256), bf16),
         vm(part, f32), vm((8, 3, ROWS, W), bf16), vm((8, ROWS, W), bf16), vm((8, 2, ROWS, W), bf16),
         vm((NZ, ROWS, W), f32), vm((NZ, ROWS, W), bf16), vm((NZ, ROWS, W), bf16),
-        vm((2, ROWS, W), bf16), vm((3, HID, W), bf16), vm((MOST_SENT, 8, 128), f32),
-        pltpu.SemaphoreType.DMA((N_PHASES,)), pltpu.SemaphoreType.DMA((N_SEMS,)), pltpu.SemaphoreType.DMA((8,)),
+        vm((MOST_SENT, 8, 128), f32),
+        pltpu.SemaphoreType.DMA((N_PHASES,)), pltpu.SemaphoreType.DMA((N_SEMS,)), pltpu.SemaphoreType.DMA((5,)),
     ]
     vmem = pl.BlockSpec(memory_space=pltpu.VMEM)
-    anywhere = pl.BlockSpec(memory_space=pl.ANY)
+    hbm = pl.BlockSpec(memory_space=pltpu.HBM)
     shapes = [jax.ShapeDtypeStruct((HID, W), bf16)] * 3 + [jax.ShapeDtypeStruct((ROWS, W), bf16)] * 2
+    args = (tokens, cotangent, gate_weight.T, up_weight.T, down_weight)
     results = pl.pallas_call(
         kernel,
         out_shape=shapes,
-        in_specs=[vmem] * 2 + [anywhere] * 3,
-        out_specs=[anywhere] * 5,
+        in_specs=[hbm] * 5,
+        out_specs=[vmem] * 5,
         scratch_shapes=scratch,
         compiler_params=pltpu.CompilerParams(
-            collective_id=0, has_side_effects=True, vmem_limit_bytes=60 * 1024 * 1024
+            collective_id=0, has_side_effects=True, vmem_limit_bytes=44 * 1024 * 1024
         ),
-    )(tokens, cotangent, gate_weight.T, up_weight.T, down_weight)
+    )(*(pltpu.with_memory_space_constraint(a, pltpu.HBM) for a in args))
     gg, ug, dg, out, ig = pl.pallas_call(
         hand_over,
         out_shape=shapes,
-        in_specs=[anywhere] * 5,
-        out_specs=[anywhere] * 5,
-        scratch_shapes=[vm(s.shape, s.dtype) for s in shapes] + [pltpu.SemaphoreType.DMA((10,))],
+        in_specs=[vmem] * 5,
+        out_specs=[hbm] * 5,
+        scratch_shapes=[pltpu.SemaphoreType.DMA((5,))],
+        compiler_params=pltpu.CompilerParams(vmem_limit_bytes=4 * 1024 * 1024),
     )(*results)
     return out, ig, gg.T, ug.T, dg
 

time: 82.3 us -> 81.2 us (0.987)
  Pallas kernels: 81.2 us -> 80.3 us
    pallas_call x2, Pallas kernels: 81.2 us -> 80.3 us  [the longest x1 79.2 us: shards(): pl.pallas_call(kernel, out_shape=shapes, in_specs=[hbm] * 5, out_specs=[v...]
where the time goes in v4:
time: 81.2 us; the launch traced here: 81.1 us
  Pallas kernels  80.3 us (99%)
    pallas_call x1, Pallas kernels, shards(): pl.pallas_call(kernel, out_shape=shapes, in_specs=[hbm] * 5, out_specs=[v...  79.2 us

profile of v4, /device:TPU:16, one launch (start us, length us, event | category | flops | bytes accessed | tf_op | source)
XLA Modules:
  0.0 81.1 jit_solution(7079511166607224671)
XLA Ops:
  0.6 79.2 %shard_map.92 = (bf16[448,512]{1,0:T(8,128)(2,1)S(1)}, bf16[448,512]{1,0:T(8,128)(2,1)S(1)}, bf16[448,512]{1,0:T(8,128)(2,1)S(1)}, bf16[32,512]{1,0:T(8,128)(2,1)S(1)}, bf16[32,512]{1,0:T(8,128)(2,1)S(1)}) custom-call(bf16[32,512]{1,0:T(8,128)(2,1)} %tok_hbm.1, bf16[32,512]{1,0:T(8,128)(2,1)} %cot_hbm.1, bf16[448,512]{1,0:T(8,128)(2,1)} %bitcast.4, ...), custom_call_target="tpu_custom_call" | custom-call | tf_op jit(solution)/shard_map/pallas_call | solution.py:774
  79.8 1.1 %shard_map.93 = (bf16[448,512]{1,0:T(8,128)(2,1)}, bf16[448,512]{1,0:T(8,128)(2,1)}, bf16[448,512]{1,0:T(8,128)(2,1)}, bf16[32,512]{1,0:T(8,128)(2,1)}, bf16[32,512]{1,0:T(8,128)(2,1)}) custom-call(bf16[448,512]{1,0:T(8,128)(2,1)S(1)} %get-tuple-element.15.refs_0_, bf16[448,512]{1,0:T(8,128)(2,1)S(1)} %get-tuple-element.16.refs_1_, ...), custom_call_target="tpu_custom_call" | custom-call | tf_op jit(solution)/shard_map/pallas_call | solution.py:784

commit v5 on v4

--- a/solution.py
+++ b/solution.py
@@ -167,8 +167,9 @@
 
 
 class ZX:
-    def __init__(self, net, own, buf, z, x):
+    def __init__(self, net, own, buf, z, x, width):
         self.net, self.own, self.buf, self.z, self.x = net, own, buf, z, x
+        self.cols = pl.ds(0, width)
         self.came, self.crossed = {}, {}
         self.far, self.relays = net.sem(), net.sem()
 
@@ -177,39 +178,74 @@
 
     def start(self):
         for d in (1, -1, 2, -2):
-            self.came[-d] = self.net.send(self.own, self.buf.at[self.z, self.x], z=self.at(d))
+            self.came[-d] = self.net.send(self.own, self.buf.at[self.z, self.x, :, self.cols], z=self.at(d))
 
     def forward(self, d):
         self.came[d].wait_recv()
         to = self.at(2 if d < 0 else -2)
-        block = self.buf.at[self.at(d), self.x]
+        block = self.buf.at[self.at(d), self.x, :, self.cols]
         if abs(d) == 1:
             self.came[3 * d] = self.net.send(block, block, z=to)
         else:
-            half = self.buf.at[self.at(d), self.x, pl.ds(0 if d < 0 else 16, 16)]
+            half = self.buf.at[self.at(d), self.x, pl.ds(0 if d < 0 else 16, 16), self.cols]
             self.net.send(half, half, self.far, z=to)
 
     def cross(self, d):
         b = self.at(d)
-        src = self.buf.at[b, self.x] if d else self.own
+        src = self.buf.at[b, self.x, :, self.cols] if d else self.own
         if abs(d) == 3:
             self.came[d].wait_recv()
         if d == 4:
-            self.net.wait(self.far, self.buf.at[0, 0])
+            self.net.wait(self.far, self.buf.at[0, 0, :, self.cols])
         self.crossed[d] = self.net.sem()
         for k in (1, 3):
-            self.net.send(src, self.buf.at[b, self.x], self.crossed[d], x=(self.x + k) % NX)
+            self.net.send(src, self.buf.at[b, self.x, :, self.cols], self.crossed[d], x=(self.x + k) % NX)
 
     def relay(self, d):
         b, xp, xm = self.at(d), (self.x + 1) % NX, (self.x + 3) % NX
-        self.net.wait(self.crossed[d], self.buf.at[0, pl.ds(0, 2)])
-        lo = self.buf.at[b, xm, pl.ds(0, 16)]
+        self.net.wait(self.crossed[d], self.buf.at[0, pl.ds(0, 2), :, self.cols])
+        lo = self.buf.at[b, xm, pl.ds(0, 16), self.cols]
         self.net.send(lo, lo, self.relays, x=xp)
-        hi = self.buf.at[b, xp, pl.ds(16, 16)]
+        hi = self.buf.at[b, xp, pl.ds(16, 16), self.cols]
         self.net.send(hi, hi, self.relays, x=xm)
 
     def done(self):
-        self.net.wait(self.relays, self.buf.at[pl.ds(0, 2)])
+        self.net.wait(self.relays, self.buf.at[pl.ds(0, 2), :, :, self.cols])
+
+
+class XZ:
+    def __init__(self, net, own, buf, z, x):
+        self.net, self.own, self.buf, self.z, self.x = net, own, buf, z, x
+        self.came = {}
+        self.near, self.far = net.sem(), net.sem()
+        self.cols = pl.ds(W - 128, 128)
+
+    def block(self, d, at=0, n=NX):
+        return self.buf.at[(self.z + d + NZ) % NZ, pl.ds(at, n), :, self.cols]
+
+    def start(self):
+        for j in (1, 3, 2):
+            dst = self.buf.at[self.z, self.x, :, self.cols]
+            self.net.send(self.own, dst, self.near, x=(self.x + j) % NX)
+
+    def second(self):
+        self.net.wait(self.near, self.buf.at[0, pl.ds(0, NX - 1), :, self.cols])
+        for d in (1, -1, 2, -2):
+            self.came[-d] = self.net.send(self.block(0), self.block(0), z=(self.z + d + NZ) % NZ)
+
+    def forward(self, d):
+        self.came[d].wait_recv()
+        to = (self.z + (2 if d < 0 else NZ - 2)) % NZ
+        if abs(d) == 1:
+            self.came[3 * d] = self.net.send(self.block(d), self.block(d), z=to)
+        else:
+            half = self.block(d, 0 if d < 0 else 2, 2)
+            self.net.send(half, half, self.far, z=to)
+
+    def done(self):
+        self.came[3].wait_recv()
+        self.came[-3].wait_recv()
+        self.net.wait(self.far, self.block(0))
 
 
 class Gather:
@@ -257,7 +293,7 @@
         self.net.wait(self.pair, self.buf.at[:, 0])
 
 
-N_SEMS = 118
+N_SEMS = 126
 N_PHASES = 5
 MOST_SENT = 1280
 RELATIVE = (3, -3, 4, 0, 2, -2, 1, -1)
@@ -332,14 +368,17 @@
     own_peaks = jnp.where(row == 0, p_x, jnp.where(row == 1, p_g, jnp.where(row == 2, p_u, p_d)))
     pl.semaphore_wait(barrier, 7 + 3 + 7)
 
-    T = ZX(net, tok, t_all, z, x)
-    C = ZX(net, cot, c_all, z, x)
+    T = ZX(net, tok.at[:, pl.ds(0, W - 128)], t_all, z, x, W - 128)
+    A = XZ(net, tok.at[:, pl.ds(W - 128, 128)], t_all, z, x)
+    C = ZX(net, cot, c_all, z, x, W)
     peaks = Peaks(net, pk_src, pk_buf, (y, c, z, x))
+    A.start()
     T.start()
     peaks.start(own_peaks)
     T.cross(0)
     T.forward(1)
     T.forward(-1)
+    A.second()
     peaks.second()
     T.cross(1)
     T.cross(-1)
@@ -347,28 +386,33 @@
         T.forward(d)
         T.cross(d)
     T.relay(0)
-    net.phase = 1
-    C.start()
+    for d in (1, -1):
+        A.forward(d)
     T.relay(1)
     T.relay(-1)
+    for d in (2, -2):
+        A.forward(d)
     T.cross(3)
     T.cross(-3)
     T.cross(4)
+    peaks.third()
+    net.phase = 1
+    C.start()
     T.relay(2)
     T.relay(-2)
-    peaks.third()
-    for d in (1, -1, 2, -2):
-        C.forward(d)
     T.relay(3)
     T.relay(-3)
     T.relay(4)
-    for d in (0, 1, -1, 2, -2):
-        C.cross(d)
     pk[...] = peaks.result()
     inv_x = 1.0 / (pk[0:1, 0:1] + TINY)
     cg[...] = (TOP * jnp.tanh(rg[...] * (1.0 / (pk[1:2, 0:1] + TINY)))).astype(bf16)
     cu[...] = (TOP * jnp.tanh(ru[...] * (1.0 / (pk[2:3, 0:1] + TINY)))).astype(bf16)
+    A.done()
     T.done()
+    for d in (1, -1, 2, -2):
+        C.forward(d)
+    for d in (0, 1, -1, 2, -2):
+        C.cross(d)
 
     def gate_up(k, dst):
         t = turn_cols(t_all[k].reshape(4 * ROWS, W), h128)
@@ -404,14 +448,14 @@
     pair_part(0)
     pair_part(1)
     own_part(0)
-    C.cross(3)
-    C.cross(-3)
-    C.cross(4)
     dh["first"].wait_recv()
     relp = put(0, q(0, 0), yrel.at[0], y=yp)
     dh[0].wait_recv()
     relm = put(1, q(0, 64), yrel.at[1], y=ym)
     own_part(1)
+    C.cross(3)
+    C.cross(-3)
+    C.cross(4)
     pair_part(2)
     C.relay(0)
     C.relay(1)

time: 81.2 us -> 81.1 us (level)
  no operation moved by 1% of the time
where the time goes in v5:
time: 81.1 us; the launch traced here: 81 us
  Pallas kernels  80.2 us (99%)
    pallas_call x1, Pallas kernels, shards(): pl.pallas_call(kernel, out_shape=shapes, in_specs=[hbm] * 5, out_specs=[v...  79.1 us

profile of v5, /device:TPU:16, one launch (start us, length us, event | category | flops | bytes accessed | tf_op | source)
XLA Modules:
  0.0 81.0 jit_solution(691285743599973584)
XLA Ops:
  0.6 79.1 %shard_map.92 = (bf16[448,512]{1,0:T(8,128)(2,1)S(1)}, bf16[448,512]{1,0:T(8,128)(2,1)S(1)}, bf16[448,512]{1,0:T(8,128)(2,1)S(1)}, bf16[32,512]{1,0:T(8,128)(2,1)S(1)}, bf16[32,512]{1,0:T(8,128)(2,1)S(1)}) custom-call(bf16[32,512]{1,0:T(8,128)(2,1)} %tok_hbm.1, bf16[32,512]{1,0:T(8,128)(2,1)} %cot_hbm.1, bf16[448,512]{1,0:T(8,128)(2,1)} %bitcast.4, ...), custom_call_target="tpu_custom_call" | custom-call | tf_op jit(solution)/shard_map/pallas_call | solution.py:818
  79.7 1.1 %shard_map.93 = (bf16[448,512]{1,0:T(8,128)(2,1)}, bf16[448,512]{1,0:T(8,128)(2,1)}, bf16[448,512]{1,0:T(8,128)(2,1)}, bf16[32,512]{1,0:T(8,128)(2,1)}, bf16[32,512]{1,0:T(8,128)(2,1)}) custom-call(bf16[448,512]{1,0:T(8,128)(2,1)S(1)} %get-tuple-element.15.refs_0_, bf16[448,512]{1,0:T(8,128)(2,1)S(1)} %get-tuple-element.16.refs_1_, ...), custom_call_target="tpu_custom_call" | custom-call | tf_op jit(solution)/shard_map/pallas_call | solution.py:828

commit v6 on v5

--- a/solution.py
+++ b/solution.py
@@ -407,10 +407,10 @@
     inv_x = 1.0 / (pk[0:1, 0:1] + TINY)
     cg[...] = (TOP * jnp.tanh(rg[...] * (1.0 / (pk[1:2, 0:1] + TINY)))).astype(bf16)
     cu[...] = (TOP * jnp.tanh(ru[...] * (1.0 / (pk[2:3, 0:1] + TINY)))).astype(bf16)
+    for d in (1, -1, 2, -2):
+        C.forward(d)
     A.done()
     T.done()
-    for d in (1, -1, 2, -2):
-        C.forward(d)
     for d in (0, 1, -1, 2, -2):
         C.cross(d)
 

time: 81.1 us -> 80.8 us (level)
  no operation moved by 1% of the time
where the time goes in v6:
time: 80.8 us; the launch traced here: 80.7 us
  Pallas kernels  79.9 us (99%)
    pallas_call x1, Pallas kernels, shards(): pl.pallas_call(kernel, out_shape=shapes, in_specs=[hbm] * 5, out_specs=[v...  78.8 us

profile of v6, /device:TPU:16, one launch (start us, length us, event | category | flops | bytes accessed | tf_op | source)
XLA Modules:
  0.0 80.7 jit_solution(16034775640950724841)
XLA Ops:
  0.6 78.8 %shard_map.92 = (bf16[448,512]{1,0:T(8,128)(2,1)S(1)}, bf16[448,512]{1,0:T(8,128)(2,1)S(1)}, bf16[448,512]{1,0:T(8,128)(2,1)S(1)}, bf16[32,512]{1,0:T(8,128)(2,1)S(1)}, bf16[32,512]{1,0:T(8,128)(2,1)S(1)}) custom-call(bf16[32,512]{1,0:T(8,128)(2,1)} %tok_hbm.1, bf16[32,512]{1,0:T(8,128)(2,1)} %cot_hbm.1, bf16[448,512]{1,0:T(8,128)(2,1)} %bitcast.4, ...), custom_call_target="tpu_custom_call" | custom-call | tf_op jit(solution)/shard_map/pallas_call | solution.py:818
  79.4 1.1 %shard_map.93 = (bf16[448,512]{1,0:T(8,128)(2,1)}, bf16[448,512]{1,0:T(8,128)(2,1)}, bf16[448,512]{1,0:T(8,128)(2,1)}, bf16[32,512]{1,0:T(8,128)(2,1)}, bf16[32,512]{1,0:T(8,128)(2,1)}) custom-call(bf16[448,512]{1,0:T(8,128)(2,1)S(1)} %get-tuple-element.15.refs_0_, bf16[448,512]{1,0:T(8,128)(2,1)S(1)} %get-tuple-element.16.refs_1_, ...), custom_call_target="tpu_custom_call" | custom-call | tf_op jit(solution)/shard_map/pallas_call | solution.py:828
